TPU v7x, 32 devices: a whole 2x2x4 slice. The times are simulated.
32 devices in a mesh: parts: 2 (over y), blk: 4 (over z), dp: 2 (over x), sub: 2 (over core).
Axes of the slice: x: 2, y: 2, z: 4, core: 2. Of those that a mesh axis runs over, the one named last changes fastest.
Arguments:
- in_factors: bfloat16 [2, 4, 512, 1024], P(None, ('parts', 'dp'), 'blk'), parts along dimension 1, may hold values from -6 to 6
- out_factors: bfloat16 [2, 4, 512, 1024], P(None, ('parts', 'dp'), 'blk'), parts along dimension 1, may hold values from -0.75 to 0.75
- lengths: int32 [4, 32], P(('parts', 'dp')), parts along dimension 0, may hold values from 1 to 64, 512 in all within a row
- signs: int32 [2, 1024, 1024], P(None, 'blk'), may hold values 0 or 1
- projection: bfloat16 [2, 1024, 16, 4096], P(None, 'blk', None, 'sub'), may hold values from -0.046875 to 0.046875
Outputs:
- features: float32 [4, 32, 2, 4096], P(('parts', 'dp'), 'blk', None, 'sub'), parts along dimension 0
There are 2 independent parts, one for each index of `parts`. A program takes and returns all parts, laid end to end along the dimension named above; an argument that names none is the same for every part. Nothing has to cross between parts.
Inputs may be any that keep to these rules, and one draw needn't show every extreme that they name: In each row the 32 lengths sum to 512; the documents follow one another over the tokens of their dp index in order.
All inputs are finite; a program needn't handle non-finite values. No bound on the sum of `signs` on one device may be relied on, other than what follows from the above.
Results may differ from a plain program's by a relative error of at most 0.0029.
Values may be sent and summed in bfloat16 or wider, within the bound.
No kernel may reach another device: no remote copies, remote signals or barrier semaphores. Data moves between devices by JAX's collectives and lax.ppermute only.
A program may use at most 128 MiB of HBM per device.

v0:
```python
import math

import jax
import jax.numpy as jnp
from jax import lax
from jax.sharding import PartitionSpec as P


def swapped(block, axis, bit):
    count = lax.axis_size(axis)
    route = []
    for low in range(count):
        high = low | 1 << bit
        if high != low and high < count:
            route += [(low, high), (high, low)]
    return lax.ppermute(block, axis, route)


def parity_sign(values):
    total = jnp.zeros_like(values)
    for bit_level in range(16):
        total = total + jnp.bitwise_and(jnp.right_shift(values, bit_level), 1)
    return (1 - 2 * (total % 2)).astype(jnp.float32)


def parity_table(row_ids, col_ids):
    return parity_sign(jnp.bitwise_and(row_ids[:, None], col_ids[None, :]))


def build_weighted(owners, example_ids, input_cols):
    one_hot = (owners[:, None] == example_ids[None, :]).astype(jnp.bfloat16)
    product = one_hot[None, :, :, None] * input_cols[:, 0, :, None, :]
    return product.reshape(product.shape[0], product.shape[1], product.shape[2] * product.shape[3])


def make_accumulate(weighted, portion):
    return jnp.einsum("ltx,ltc->lxc", weighted, portion[:, 0], preferred_element_type=jnp.float32)


def shards(in_factors, out_factors, lengths, signs, projection):
    blocks = lax.axis_size("blk")
    halves = lax.axis_size("sub")
    my_block = lax.axis_index("blk")
    my_half = lax.axis_index("sub")
    layers = in_factors.shape[0]
    tok_local = in_factors.shape[2]
    in_width = in_factors.shape[3]
    out_width = out_factors.shape[3]
    rows_block = in_width // blocks
    documents = lengths.shape[1]
    kept_cols = projection.shape[2]
    tok_shard = tok_local * blocks
    norm_scale = 1.0 / math.sqrt(in_width * out_width)
    input_cols = lax.all_to_all(in_factors, "blk", split_axis=3, concat_axis=2, tiled=True)
    doc_ends = jnp.cumsum(lengths[0])
    positions = jnp.arange(tok_shard, dtype=jnp.int32)
    owners = jnp.sum((positions[:, None] >= doc_ends[None, :]).astype(jnp.int32), axis=1)
    width_part = out_width // halves
    col_base = my_half * width_part
    example_ids = jnp.arange(documents, dtype=jnp.int32)
    right_part = lax.dynamic_slice_in_dim(out_factors, col_base, width_part, 3)
    weighted = build_weighted(owners, example_ids, input_cols)
    gradients = make_accumulate(weighted, lax.all_gather(right_part, "blk", axis=2, tiled=True))
    gradients = gradients.reshape(layers, documents, rows_block, width_part)
    col_ids = col_base + jnp.arange(width_part, dtype=jnp.int32)
    sign_slice = lax.dynamic_slice_in_dim(signs, col_base, width_part, 2)
    signed = (2 * sign_slice - 1).astype(jnp.float32)
    col_mix = parity_table(col_ids, jnp.arange(kept_cols, dtype=jnp.int32))
    mixing = signed[:, :, :, None] * col_mix[None, None, :, :]
    folded = jnp.einsum("leic,lick->leik", gradients, mixing, precision=lax.Precision.HIGHEST)
    local_rows = jnp.arange(rows_block, dtype=jnp.int32)
    row_mix = parity_table(local_rows, local_rows)
    within = jnp.einsum("ji,leik->lejk", row_mix, folded, precision=lax.Precision.HIGHEST)
    within = within.reshape(layers, documents, rows_block * kept_cols)
    within = lax.psum_scatter(within, "sub", scatter_dimension=1, tiled=True)
    blended = within
    for bit_level in range(blocks.bit_length() - 1):
        partner = swapped(blended, "blk", bit_level)
        high_bit = jnp.bitwise_and(jnp.right_shift(my_block, bit_level), 1)
        blended = partner + (1 - 2 * high_bit).astype(jnp.float32) * blended
    kept_half = (blended * norm_scale).astype(jnp.bfloat16)
    gathered = lax.all_gather(kept_half, "sub", axis=1, tiled=True)
    weights = projection.reshape(layers, rows_block * kept_cols, projection.shape[3])
    features = lax.psum_scatter(
        jnp.einsum("lek,lkp->elp", gathered, weights, preferred_element_type=jnp.float32),
        "blk",
        scatter_dimension=0,
        tiled=True,
    )
    return features[None]


def solution(mesh):
    return jax.shard_map(
        shards,
        mesh=mesh,
        in_specs=(
            P(None, ("parts", "dp"), "blk", None),
            P(None, ("parts", "dp"), "blk", None),
            P(("parts", "dp"), None),
            P(None, "blk", None),
            P(None, "blk", None, "sub"),
        ),
        out_specs=P(("parts", "dp"), "blk", None, "sub"),
        check_vma=False,
    )
```

profile of v0, /device:TPU:0, one launch (start us, length us, event | category | flops | bytes accessed | tf_op | source)
XLA Modules:
  0.0 233.8 jit_solution(1665426962694286551)
XLA Ops:
  6.5 0.0 copy-start
  6.5 0.0 all-gather.2.cloned.1.call-start
  6.5 1.0 copy-done
  7.6 0.7 constant_dynamic-slice_fusion
  8.3 0.0 all-gather.2.cloned.1.call-update
  8.3 2.0 copy.37
  10.3 6.3 %all-to-all-start = ((bf16[2,1,128,1024]{2,0,1,3:T(2,128)(2,1)}), bf16[2,1,128,1024]{2,0,1,3:T(2,128)(2,1)S(1)}, u32[]{:S(2)}, u32[]{:S(2)}) async-start(bf16[2,1,128,1024]{2,0,1,3:T(2,128)(2,1)} %copy.37), calls=%async_computation | async-start | bytes 1048576 | tf_op jit(solution)/shard_map/all_to_all | solution.py:54
  16.7 0.0 reduce-scatter.3.cloned.1.call-start
  16.7 0.7 copy.36
  17.4 0.1 reduce-window.8
  17.5 0.1 reduce
  17.6 0.1 convert_reduce_fusion
  17.7 1.4 add_convert_fusion
  19.1 0.1 fusion.41
  19.2 24.0 %all-to-all-done = bf16[2,1,128,1024]{2,0,1,3:T(2,128)(2,1)S(1)} async-done(((bf16[2,1,128,1024]{2,0,1,3:T(2,128)(2,1)}), bf16[2,1,128,1024]{2,0,1,3:T(2,128)(2,1)S(1)}, u32[]{:S(2)}, u32[]{:S(2)}) %all-to-all-start) | async-done | bytes 524320 | tf_op jit(solution)/shard_map/all_to_all | solution.py:54
  43.2 0.1 copy.38
  43.3 0.2 copy.39
  43.5 0.2 copy.40
  43.7 0.6 mul.85
  44.4 7.6 %bitcast_multiply_fusion = bf16[2,512,8192]{1,2,0:T(8,128)(2,1)} fusion(bf16[2,512,256]{1,2,0:T(8,128)(2,1)S(1)} %copy.40, bf16[512,8192]{0,1:T(8,128)(2,1)S(1)} %bitcast.34), kind=kLoop, calls=%fused_computation.2 | loop fusion | flops 8388608 | bytes 25690112 | tf_op jit(solution)/shard_map/mul | solution.py:32
  51.9 0.0 all-gather.2.cloned.1.call-done
  51.9 18.9 %fusion.10 = f32[2,8192,512]{2,1,0:T(8,128)} fusion(bf16[2,512,8192]{1,2,0:T(8,128)(2,1)} %bitcast_multiply_fusion, bf16[2,1,512,512]{3,2,0,1:T(8,128)(2,1)} %all-gather.2.cloned.1.call-done), kind=kOutput, calls=%fused_computation.9 | convolution fusion | flops 8589934592 | bytes 51380224 | tf_op jit(solution)/shard_map/ltx,ltc->lxc/dot_general | solution.py:37
  70.8 54.3 %fusion.5 = f32[2,32,256,16]{1,3,2,0:T(8,128)} fusion(f32[2,32,256,512]{3,2,1,0:T(8,128)} %bitcast.32, f32[512,16]{0,1:T(8,128)S(1)} %fusion.41, f32[2,256,512]{2,1,0:T(8,128)S(1)} %add_convert_fusion), kind=kOutput, calls=%fused_computation.7 | convolution fusion | flops 1614807040 | bytes 35684352 | tf_op jit(solution)/shard_map/leic,lick->leik/dot_general | solution.py:70
  125.1 4.0 %copy.43 = f32[2,32,256,16]{2,3,1,0:T(8,128)S(1)} copy(f32[2,32,256,16]{1,3,2,0:T(8,128)} %fusion.5) | data formatting | bytes 2097152 | tf_op jit(solution)/shard_map/leic,lick->leik/transpose | solution.py:70
  129.1 1.5 convolution_bitcast_fusion.1
  130.7 3.9 %copy.44 = f32[2,32,256,16]{1,3,2,0:T(8,128)} copy(f32[2,32,256,16]{2,3,1,0:T(8,128)S(1)} %convolution_bitcast_fusion.1) | data formatting | bytes 2097152 | tf_op jit(solution)/shard_map/ji,leik->lejk/transpose | solution.py:73
  134.5 3.6 %copy.45 = f32[2,32,4096]{2,1,0:T(8,128)} copy(f32[2,32,4096]{1,2,0:T(8,128)} %bitcast.35) | data formatting | bytes 2097152 | tf_op jit(solution)/shard_map/reshape | solution.py:74
  138.1 0.0 reduce-scatter.3.cloned.1.call-update
  138.2 0.0 reduce-scatter.5.cloned.1.call-start
  138.2 6.7 %reduce-scatter.3.cloned.1.call-done = f32[2,16,4096]{2,1,0:T(8,128)} async-done(((f32[2,32,4096]{2,1,0:T(8,128)}), f32[2,16,4096]{2,1,0:T(8,128)}) %reduce-scatter.3.cloned.1.call-update) | async-done | bytes 524304 | tf_op jit(solution)/shard_map/reduce_scatter | solution.py:75
  145.0 1.8 collective-permute-start
  146.8 12.5 %collective-permute-done = f32[2,16,4096]{2,1,0:T(8,128)S(1)} collective-permute-done((f32[2,16,4096]{2,1,0:T(8,128)}, f32[2,16,4096]{2,1,0:T(8,128)S(1)}, u32[]{:S(2)}, u32[]{:S(2)}) %collective-permute-start) | collective-permute-done | bytes 524320 | tf_op jit(solution)/shard_map/ppermute | solution.py:16
  159.3 1.1 multiply_add_fusion
  160.4 2.7 %collective-permute-start.1 = (f32[2,16,4096]{2,1,0:T(8,128)S(1)}, f32[2,16,4096]{2,1,0:T(8,128)S(1)}, u32[]{:S(2)}, u32[]{:S(2)}) collective-permute-start(f32[2,16,4096]{2,1,0:T(8,128)S(1)} %multiply_add_fusion), channel_id=1, source_target_pairs={{0,8},{8,0},{4,12},{12,4},{1,9},{9,1},{5,13},{13,5},{2,10},{10,2},... | collective-permute-start | bytes 1572872 | tf_op jit(solution)/shard_map/ppermute | solution.py:16
  163.1 22.8 %collective-permute-done.1 = f32[2,16,4096]{2,1,0:T(8,128)S(1)} collective-permute-done((f32[2,16,4096]{2,1,0:T(8,128)S(1)}, f32[2,16,4096]{2,1,0:T(8,128)S(1)}, u32[]{:S(2)}, u32[]{:S(2)}) %collective-permute-start.1) | collective-permute-done | bytes 524320 | tf_op jit(solution)/shard_map/ppermute | solution.py:16
  185.9 0.1 multiply_convert_fusion
  185.9 2.2 all_gather.7
  188.1 0.0 copy-start.1
  188.1 14.4 %convolution_bitcast_fusion = f32[32,2,2048]{2,0,1:T(8,128)} fusion(bf16[2,32,4096]{2,1,0:T(8,128)(2,1)S(1)} %all_gather.7, bf16[2,4096,2048]{2,1,0:T(8,128)(2,1)} %bitcast.33), kind=kOutput, calls=%fused_computation.6 | convolution fusion | flops 1073741824 | bytes 34603008 | tf_op jit(solution)/shard_map/lek,lkp->elp/dot_general | solution.py:85
  202.5 0.0 reduce-scatter.5.cloned.1.call-update
  202.5 23.1 %reduce-scatter.5.cloned.1.call-done = f32[8,2,2048]{2,0,1:T(8,128)} async-done(((f32[32,2,2048]{2,0,1:T(8,128)}), f32[8,2,2048]{2,0,1:T(8,128)}) %reduce-scatter.5.cloned.1.call-update) | async-done | bytes 131088 | tf_op jit(solution)/shard_map/reduce_scatter | solution.py:84
  225.6 1.7 copy.46
  227.3 0.0 copy-done.1
  (2 shorter events, 0.0 us)
Async XLA Ops:
  6.5 1.0 copy-start
  6.5 45.4 %all-gather.2.cloned.1.call-start = ((), (), s32[]{:S(2)}) async-start(), calls=%async_computation.3 | async-start | bytes 1310720 | tf_op jit(solution)/shard_map/all_gather | solution.py:63
  10.3 32.9 %all-to-all-start = ((bf16[2,1,128,1024]{2,0,1,3:T(2,128)(2,1)}), bf16[2,1,128,1024]{2,0,1,3:T(2,128)(2,1)S(1)}, u32[]{:S(2)}, u32[]{:S(2)}) async-start(bf16[2,1,128,1024]{2,0,1,3:T(2,128)(2,1)} %copy.37), calls=%async_computation | async-start | bytes 1048576 | tf_op jit(solution)/shard_map/all_to_all | solution.py:54
  16.7 128.3 %reduce-scatter.3.cloned.1.call-start = ((), (), s32[]{:S(2)}) async-start(), calls=%async_computation.4 | async-start | bytes 1572864 | tf_op jit(solution)/shard_map/reduce_scatter | solution.py:75
  138.2 87.4 %reduce-scatter.5.cloned.1.call-start = ((), (), s32[]{:S(2)}) async-start(), calls=%async_computation.5 | async-start | bytes 655360 | tf_op jit(solution)/shard_map/reduce_scatter | solution.py:84
  145.0 14.3 %collective-permute-start = (f32[2,16,4096]{2,1,0:T(8,128)}, f32[2,16,4096]{2,1,0:T(8,128)S(1)}, u32[]{:S(2)}, u32[]{:S(2)}) collective-permute-start(f32[2,16,4096]{2,1,0:T(8,128)} %reduce-scatter.3.cloned.1.call-done), channel_id=1, source_target_pairs={{0,4},{4,0},{8,12},{12,8},{1,5},{5,1},{9,13},{13,9},{2,6},{6,2},{1... | collective-permute-start | bytes 1572872 | tf_op jit(solution)/shard_map/ppermute | solution.py:16
  160.4 25.5 %collective-permute-start.1 = (f32[2,16,4096]{2,1,0:T(8,128)S(1)}, f32[2,16,4096]{2,1,0:T(8,128)S(1)}, u32[]{:S(2)}, u32[]{:S(2)}) collective-permute-start(f32[2,16,4096]{2,1,0:T(8,128)S(1)} %multiply_add_fusion), channel_id=1, source_target_pairs={{0,8},{8,0},{4,12},{12,4},{1,9},{9,1},{5,13},{13,5},{2,10},{10,2},... | collective-permute-start | bytes 1572872 | tf_op jit(solution)/shard_map/ppermute | solution.py:16
  188.1 39.1 %copy-start.1 = (bf16[2,1,128,1024]{3,2,1,0:T(8,128)(2,1)S(1)}, bf16[2,1,128,1024]{3,2,1,0:T(8,128)(2,1)}, u32[]{:S(2)}) copy-start(bf16[2,1,128,1024]{3,2,1,0:T(8,128)(2,1)} %param.6) | copy-start | bytes 1572868
Sparse Core Ops, SparseCore 0:
  8.9 39.3 all-gather.1
  138.3 6.6 reduce-scatter.2
  202.6 22.9 reduce-scatter.4
where the time goes:
time: 234 us
  waiting for transfers between devices  89.2 us (38%)
  matrix products  89.1 us (38%)
  local copies, waits for them, and re-layouts  18.8 us (8%)
  between operations  13.2 us (6%)
  starting transfers between devices  10.9 us (5%)
  other arithmetic  10.5 us (4%)
    dot_general x1, matrix products, shards(): jnp.einsum('leic,lick->leik', gradients, mixing, precision=lax.Precision....  54.3 us
    ppermute x2, waiting for transfers between devices, swapped(): return lax.ppermute(block, axis, route)  35.3 us
    all_to_all x1, waiting for transfers between devices, shards(): lax.all_to_all(in_factors, 'blk', split_axis=3, concat_axis=2, tiled=True)  24 us
    reduce_scatter x1, waiting for transfers between devices, shards(): lax.psum_scatter(jnp.einsum('lek,lkp->elp', gathered, weights, preferred_...  23.1 us
    dot_general x1, matrix products, make_accumulate(): jnp.einsum('ltx,ltc->lxc', weighted, portion[:, 0], preferred_element_typ...  18.9 us
    dot_general x1, matrix products, shards(): jnp.einsum('lek,lkp->elp', gathered, weights, preferred_element_type=jnp....  14.4 us
    mul x1, other arithmetic, build_weighted(): product = one_hot[None, :, :, None] * input_cols[:, 0, :, None, :]  7.57 us
    reduce_scatter x1, waiting for transfers between devices, shards(): within = lax.psum_scatter(within, 'sub', scatter_dimension=1, tiled=True)  6.74 us
  transfers between devices with their start and end apart: 6, of which 5 were waited for; matrix products, arithmetic and copies ran while one was open for 6% of the time, Pallas kernels for 0%

commit v1 on v0

v1 whole, which is shorter than its diff:
```python
import functools
import math

import jax
import jax.numpy as jnp
from jax import lax
from jax.experimental import pallas as pl
from jax.experimental.pallas import tpu as pltpu
from jax.sharding import PartitionSpec as P

F32 = jnp.float32
BF16 = jnp.bfloat16
NT = (((1,), (1,)), ((), ()))


def parity_sign(values):
    for shift in (8, 4, 2, 1):
        values = jnp.bitwise_xor(values, jnp.right_shift(values, shift))
    return (1 - 2 * jnp.bitwise_and(values, 1)).astype(F32)


def iota(shape, dim):
    return lax.broadcasted_iota(jnp.int32, shape, dim)


def split_bf16(x):
    hi = x.astype(BF16)
    return hi, (x - hi.astype(F32)).astype(BF16)


def fold_kernel(blocks, kept, ids_ref, lengths_ref, signs_ref, left_ref, *refs):
    own_ref = refs[0]
    up_refs = refs[1:blocks]
    down_refs = refs[blocks:2 * blocks - 1]
    out_ref, b_scr, a_scr, h_scr, hot_scr = refs[2 * blocks - 1:]
    tokens, width = b_scr.shape
    tok_local = tokens // blocks
    documents = hot_scr.shape[0]
    me = ids_ref[1]

    @pl.when(pl.program_id(0) == 0)
    def _():
        def place(ref, block):
            b_scr[pl.ds(pl.multiple_of(block * tok_local, tok_local), tok_local), :] = ref[...]

        place(own_ref, me)
        for step in range(1, blocks):
            pl.when(me - step >= 0)(functools.partial(place, up_refs[step - 1], me - step))
            pl.when(me + step < blocks)(functools.partial(place, down_refs[step - 1], me + step))
        for block in range(blocks):
            a_scr[:, block * tok_local:(block + 1) * tok_local] = left_ref[block].astype(F32)
        h_scr[...] = parity_sign(jnp.bitwise_and(iota(h_scr.shape, 0), iota(h_scr.shape, 1)))
        square = (documents, documents)
        spread = jnp.broadcast_to(lengths_ref[...].astype(F32), square)
        ends = jnp.sum(jnp.where(iota(square, 1) <= iota(square, 0), spread, 0.0), axis=1, keepdims=True)
        starts = jnp.sum(jnp.where(iota(square, 1) < iota(square, 0), spread, 0.0), axis=1, keepdims=True)
        token = iota((documents, tokens), 1).astype(F32)
        hot = jnp.where((token >= starts) & (token < ends), 1.0, 0.0).astype(BF16)
        hot_scr[:, :tokens] = hot
        hot_scr[:, tokens:] = hot

    rows = signs_ref.shape[1]
    row0 = pl.multiple_of(pl.program_id(0) * rows, rows)
    signed = (2 * signs_ref[0] - 1).astype(F32)
    mixing = (signed[:, None, :] * h_scr[...][None]).reshape(rows * kept, width).astype(BF16)
    mixed = lax.dot_general(mixing, b_scr[...], NT, preferred_element_type=F32)
    left = a_scr[pl.ds(row0, rows), :]
    terms = (mixed.reshape(rows, kept, tokens) * left[:, None, :]).reshape(rows * kept, tokens)
    hi, lo = split_bf16(terms)
    out_ref[...] = lax.dot_general(
        hot_scr[...], jnp.concatenate([hi, lo], axis=1), NT, preferred_element_type=F32
    )


def fold(ids, lengths, signs, left, own, up, down, kept):
    blocks, rows_block, tok_local = left.shape
    width = own.shape[1]
    tokens = blocks * tok_local
    documents = lengths.shape[1]
    rows = min(16, rows_block)
    whole = lambda shape: pl.BlockSpec(shape, lambda g, ids: (0,) * len(shape))
    return pl.pallas_call(
        functools.partial(fold_kernel, blocks, kept),
        grid_spec=pltpu.PrefetchScalarGridSpec(
            num_scalar_prefetch=1,
            grid=(rows_block // rows,),
            in_specs=[
                whole(lengths.shape),
                pl.BlockSpec((1, rows, width), lambda g, ids: (ids[0], g, 0)),
                whole(left.shape),
            ] + [whole(own.shape)] * (2 * blocks - 1),
            out_specs=pl.BlockSpec((documents, rows * kept), lambda g, ids: (0, g)),
            scratch_shapes=[
                pltpu.VMEM((tokens, width), BF16),
                pltpu.VMEM((rows_block, tokens), F32),
                pltpu.VMEM((kept, width), F32),
                pltpu.VMEM((documents, 2 * tokens), BF16),
            ],
        ),
        out_shape=jax.ShapeDtypeStruct((documents, rows_block * kept), F32),
        name="fold",
    )(ids, lengths, signs, left, own, *up, *down)


def mix_kernel(blocks, kept, scale, in_ref, out_ref):
    rows, lanes = in_ref.shape
    docs = rows // blocks
    tile = min(256, lanes)
    count = lanes // tile
    row, col = iota((tile, tile), 0), iota((tile, tile), 1)
    same = jnp.bitwise_and(row, kept - 1) == jnp.bitwise_and(col, kept - 1)
    table = parity_sign(jnp.bitwise_and(row // kept, col // kept))
    table = jnp.where(same, table, 0.0).astype(BF16)
    stacked = jnp.concatenate([in_ref[:, t * tile:(t + 1) * tile] for t in range(count)], axis=0)
    hi, lo = split_bf16(stacked)
    both = jnp.dot(jnp.concatenate([hi, lo], axis=0), table, preferred_element_type=F32)
    both = both[:count * rows] + both[count * rows:]
    parts = [[both[t * rows + b * docs:t * rows + (b + 1) * docs] for b in range(blocks)] for t in range(count)]

    def butterfly(items):
        step = 1
        while step < len(items):
            for low in range(len(items)):
                if not low & step:
                    a, b = items[low], items[low | step]
                    items[low], items[low | step] = a + b, a - b
            step *= 2
        return items

    for b in range(blocks):
        column = butterfly([parts[t][b] for t in range(count)])
        for t in range(count):
            parts[t][b] = column[t]
    for t in range(count):
        done = butterfly(parts[t])
        for b in range(blocks):
            out_ref[b * docs:(b + 1) * docs, t * tile:(t + 1) * tile] = (done[b] * scale).astype(BF16)


def mix(folded, blocks, kept, scale):
    return pl.pallas_call(
        functools.partial(mix_kernel, blocks, kept, scale),
        out_shape=jax.ShapeDtypeStruct(folded.shape, BF16),
        name="mix",
    )(folded)


def project_kernel(ids_ref, kept_ref, weights_ref, out_ref, acc_ref):
    step = pl.program_id(0)

    @pl.when(step == 0)
    def _():
        acc_ref[...] = jnp.zeros_like(acc_ref)

    acc_ref[...] += jnp.dot(kept_ref[...], weights_ref[0], preferred_element_type=F32)

    @pl.when(step == pl.num_programs(0) - 1)
    def _():
        out_ref[...] = acc_ref[...].astype(out_ref.dtype)


def project(layer, kept, weights):
    documents, depth = kept.shape
    width = weights.shape[2]
    part = min(512, depth)
    return pl.pallas_call(
        project_kernel,
        grid_spec=pltpu.PrefetchScalarGridSpec(
            num_scalar_prefetch=1,
            grid=(depth // part,),
            in_specs=[
                pl.BlockSpec((documents, part), lambda g, ids: (0, g)),
                pl.BlockSpec((1, part, width), lambda g, ids: (ids[0], g, 0)),
            ],
            out_specs=pl.BlockSpec((documents, width), lambda g, ids: (0, 0)),
            scratch_shapes=[pltpu.VMEM((documents, width), F32)],
        ),
        out_shape=jax.ShapeDtypeStruct((documents, width), BF16),
        name="project",
        cost_estimate=pl.CostEstimate(
            flops=2 * documents * depth * width, bytes_accessed=2 * depth * width, transcendentals=0
        ),
    )(layer, kept, weights)


def line(block, count, step):
    return lax.ppermute(block, "blk", [(i, i + step) for i in range(count) if 0 <= i + step < count])


def exchange(rows):
    return lax.all_to_all(rows, "blk", split_axis=0, concat_axis=0, tiled=True)


def shards(in_factors, out_factors, lengths, signs, projection):
    blocks = lax.axis_size("blk")
    halves = lax.axis_size("sub")
    my_block = lax.axis_index("blk")
    my_half = lax.axis_index("sub")
    layers, _, tok_local, in_width = in_factors.shape
    out_width = out_factors.shape[3]
    assert layers == halves == 2
    rows_block = in_width // blocks
    documents = lengths.shape[1]
    docs = documents // blocks
    kept_cols = projection.shape[2]
    scale = 1.0 / math.sqrt(in_width * out_width)

    own = lax.dynamic_index_in_dim(out_factors[:, 0], my_half, 0, keepdims=False)
    left = lax.dynamic_index_in_dim(in_factors[:, 0], my_half, 0, keepdims=False)
    left = exchange(left.T.reshape(blocks, rows_block, tok_local))
    up, down = [], []
    for step in range(1, blocks):
        up.append(line(up[-1] if up else own, blocks, 1))
        down.append(line(down[-1] if down else own, blocks, -1))
    ids = jnp.stack([my_half, my_block]).astype(jnp.int32)
    folded = fold(ids, lengths, signs, left, own, up, down, kept_cols)
    folded = exchange(folded)
    kept = exchange(mix(folded, blocks, kept_cols, scale))
    other = lax.ppermute(kept, "sub", [(0, 1), (1, 0)])
    weights = projection.reshape(layers, rows_block * kept_cols, projection.shape[3])
    width = weights.shape[2]
    mine = project(ids[:1], kept, weights)
    theirs = project(1 - ids[:1], other, weights)
    mine = exchange(mine).reshape(blocks, docs, width).astype(F32)
    theirs = exchange(theirs).reshape(blocks, docs, width).astype(F32)
    mine, theirs = jnp.sum(mine, axis=0), jnp.sum(theirs, axis=0)
    first = my_half == 0
    return jnp.stack([jnp.where(first, mine, theirs), jnp.where(first, theirs, mine)], axis=1)[None]


def solution(mesh):
    return jax.shard_map(
        shards,
        mesh=mesh,
        in_specs=(
            P(None, ("parts", "dp"), "blk", None),
            P(None, ("parts", "dp"), "blk", None),
            P(("parts", "dp"), None),
            P(None, "blk", None),
            P(None, "blk", None, "sub"),
        ),
        out_specs=P(("parts", "dp"), "blk", None, "sub"),
        check_vma=False,
    )
```

time: 234 us -> 124 us (0.53)
  matrix products: 89.1 us -> 0 us
  waiting for transfers between devices: 89.2 us -> 16.9 us
  Pallas kernels: 0 us -> 38.9 us
  blocking collectives: 2.18 us -> 28.4 us
  starting transfers between devices: 10.9 us -> 31.5 us
  local copies, waits for them, and re-layouts: 18.8 us -> 5.06 us
  between operations: 13.2 us -> 0.21 us
  other arithmetic: 10.5 us -> 1.45 us
    dot_general x4 -> x0, matrix products: 89.1 us -> none  [the longest x1 54.3 us: shards(): jnp.einsum('leic,lick->leik', gradients, mixing, precision=lax.Precision....]
    pallas_call x0 -> x4, Pallas kernels: none -> 38.9 us  [the longest x2 20.2 us: project(): pl.pallas_call(project_kernel, grid_spec=pltpu.PrefetchScalarGridSpec(num...]
    reduce_scatter x2 -> x0, waiting for transfers between devices: 29.8 us -> none  [the longest x1 23.1 us: shards(): lax.psum_scatter(jnp.einsum('lek,lkp->elp', gathered, weights, preferred_...]
    all_to_all x0 -> x2, blocking collectives: none -> 28.4 us  [exchange(): return lax.all_to_all(rows, 'blk', split_axis=0, concat_axis=0, tiled=True)]
    ppermute x2 -> x7, waiting for transfers between devices: 35.3 us -> 9.75 us  [the longest x6 9.75 us: line(): lax.ppermute(block, 'blk', [(i, i + step) for i in range(count) if 0 <= i...]
    all_to_all x1 -> x3, waiting for transfers between devices: 24 us -> 7.12 us  [exchange(): return lax.all_to_all(rows, 'blk', split_axis=0, concat_axis=0, tiled=True)]
    ppermute x2 -> x7, starting transfers between devices: 4.52 us -> 17.2 us  [the longest x6 17.2 us: line(): lax.ppermute(block, 'blk', [(i, i + step) for i in range(count) if 0 <= i...]
    all_to_all x1 -> x3, starting transfers between devices: 6.35 us -> 14.3 us  [exchange(): return lax.all_to_all(rows, 'blk', split_axis=0, concat_axis=0, tiled=True)]
  transfers between devices with their start and end apart: 6 -> 10, of which waited for: 5 -> 5; matrix products, arithmetic and copies ran while one was open for 6% -> 2% of each run, Pallas kernels for 0% -> 17%
where the time goes in v1:
time: 124 us; the launch traced here: 122 us
  Pallas kernels  38.9 us (31%)
  starting transfers between devices  31.5 us (25%)
  blocking collectives  28.4 us (23%)
  waiting for transfers between devices  16.9 us (14%)
  local copies, waits for them, and re-layouts  5.06 us (4%)
  other arithmetic  1.45 us (1%)
    all_to_all x2, blocking collectives, exchange(): return lax.all_to_all(rows, 'blk', split_axis=0, concat_axis=0, tiled=True)  28.4 us
    pallas_call x2, Pallas kernels, project(): pl.pallas_call(project_kernel, grid_spec=pltpu.PrefetchScalarGridSpec(num...  20.2 us
    ppermute x6, starting transfers between devices, line(): lax.ppermute(block, 'blk', [(i, i + step) for i in range(count) if 0 <= i...  17.2 us
    pallas_call x1, Pallas kernels, fold(): pl.pallas_call(functools.partial(fold_kernel, blocks, kept), grid_spec=pl...  16.4 us
    all_to_all x3, starting transfers between devices, exchange(): return lax.all_to_all(rows, 'blk', split_axis=0, concat_axis=0, tiled=True)  14.3 us
    ppermute x6, waiting for transfers between devices, line(): lax.ppermute(block, 'blk', [(i, i + step) for i in range(count) if 0 <= i...  9.75 us
    all_to_all x3, waiting for transfers between devices, exchange(): return lax.all_to_all(rows, 'blk', split_axis=0, concat_axis=0, tiled=True)  7.12 us
    unnamed x22, local copies, waits for them, and re-layouts  3.13 us
  transfers between devices with their start and end apart: 10, of which 5 were waited for; matrix products, arithmetic and copies ran while one was open for 2% of the time, Pallas kernels for 17%

profile of v1, /device:TPU:0, one launch (start us, length us, event | category | flops | bytes accessed | tf_op | source)
XLA Modules:
  0.0 122.3 jit_solution(16665483731587025735)
XLA Ops:
  0.0 0.0 copy-start
  0.0 1.0 copy-done
  1.1 0.0 copy-start.2
  1.1 5.0 %collective-permute-start = (bf16[128,1024]{1,0:T(8,128)(2,1)S(1)}, bf16[128,1024]{1,0:T(8,128)(2,1)S(1)}, u32[]{:S(2)}, u32[]{:S(2)}) collective-permute-start(bf16[128,1024]{1,0:T(8,128)(2,1)S(1)} %dynamic-slice_bitcast_fusion.refs_0_), channel_id=1, source_target_pairs={{0,4},{4,8},{8,12},{1,5},{5,9},{9,13},{2,6},{6,10},{10,14},{3,7},{... | collective-permute-start | bytes 786440 | tf_op jit(solution)/shard_map/ppermute | solution.py:187
  6.1 1.3 %collective-permute-start.3 = (bf16[128,1024]{1,0:T(8,128)(2,1)S(1)}, bf16[128,1024]{1,0:T(8,128)(2,1)S(1)}, u32[]{:S(2)}, u32[]{:S(2)}) collective-permute-start(bf16[128,1024]{1,0:T(8,128)(2,1)S(1)} %dynamic-slice_bitcast_fusion.refs_0_), channel_id=1, source_target_pairs={{4,0},{8,4},{12,8},{5,1},{9,5},{13,9},{6,2},{10,6},{14,10},{7,3},{... | collective-permute-start | bytes 786440 | tf_op jit(solution)/shard_map/ppermute | solution.py:187
  7.4 4.2 %collective-permute-done.refs_1_ = bf16[128,1024]{1,0:T(8,128)(2,1)S(1)} collective-permute-done((bf16[128,1024]{1,0:T(8,128)(2,1)S(1)}, bf16[128,1024]{1,0:T(8,128)(2,1)S(1)}, u32[]{:S(2)}, u32[]{:S(2)}) %collective-permute-start) | collective-permute-done | bytes 262176 | tf_op jit(solution)/shard_map/ppermute | solution.py:187
  11.6 4.4 %collective-permute-start.1 = (bf16[128,1024]{1,0:T(8,128)(2,1)S(1)}, bf16[128,1024]{1,0:T(8,128)(2,1)S(1)}, u32[]{:S(2)}, u32[]{:S(2)}) collective-permute-start(bf16[128,1024]{1,0:T(8,128)(2,1)S(1)} %collective-permute-done.refs_1_), channel_id=1, source_target_pairs={{0,4},{4,8},{8,12},{1,5},{5,9},{9,13},{2,6},{6,10},{10,14},{3,7},{... | collective-permute-start | bytes 786440 | tf_op jit(solution)/shard_map/ppermute | solution.py:187
  16.0 0.0 collective-permute-done.3.refs_4_
  16.0 0.0 copy-start.6
  16.0 1.3 %collective-permute-start.4 = (bf16[128,1024]{1,0:T(8,128)(2,1)S(1)}, bf16[128,1024]{1,0:T(8,128)(2,1)S(1)}, u32[]{:S(2)}, u32[]{:S(2)}) collective-permute-start(bf16[128,1024]{1,0:T(8,128)(2,1)S(1)} %collective-permute-done.3.refs_4_), channel_id=1, source_target_pairs={{4,0},{8,4},{12,8},{5,1},{9,5},{13,9},{6,2},{10,6},{14,10},{7,3},{... | collective-permute-start | bytes 786440 | tf_op jit(solution)/shard_map/ppermute | solution.py:187
  17.3 1.0 dynamic-slice_bitcast_fusion.1
  18.3 0.8 copy.7
  19.1 5.9 %all-to-all-start = ((bf16[4,256,128]{2,1,0:T(8,128)(2,1)}), bf16[4,256,128]{2,1,0:T(8,128)(2,1)S(1)}, u32[]{:S(2)}, u32[]{:S(2)}) async-start(bf16[4,256,128]{2,1,0:T(8,128)(2,1)} %bitcast.4), calls=%async_computation | async-start | bytes 524288 | tf_op jit(solution)/shard_map/all_to_all | solution.py:191
  25.0 0.0 collective-permute-done.1.refs_2_
  25.1 3.9 %collective-permute-start.2 = (bf16[128,1024]{1,0:T(8,128)(2,1)S(1)}, bf16[128,1024]{1,0:T(8,128)(2,1)S(1)}, u32[]{:S(2)}, u32[]{:S(2)}) collective-permute-start(bf16[128,1024]{1,0:T(8,128)(2,1)S(1)} %collective-permute-done.1.refs_2_), channel_id=1, source_target_pairs={{0,4},{4,8},{8,12},{1,5},{5,9},{9,13},{2,6},{6,10},{10,14},{3,7},{... | collective-permute-start | bytes 786440 | tf_op jit(solution)/shard_map/ppermute | solution.py:187
  29.0 0.0 collective-permute-done.4.refs_5_
  29.0 0.0 copy-start.8
  29.0 1.3 %collective-permute-start.5 = (bf16[128,1024]{1,0:T(8,128)(2,1)S(1)}, bf16[128,1024]{1,0:T(8,128)(2,1)S(1)}, u32[]{:S(2)}, u32[]{:S(2)}) collective-permute-start(bf16[128,1024]{1,0:T(8,128)(2,1)S(1)} %collective-permute-done.4.refs_5_), channel_id=1, source_target_pairs={{4,0},{8,4},{12,8},{5,1},{9,5},{13,9},{6,2},{10,6},{14,10},{7,3},{... | collective-permute-start | bytes 786440 | tf_op jit(solution)/shard_map/ppermute | solution.py:187
  30.3 0.6 pad_add_fusion.ids_ref
  30.9 1.2 all-to-all-done.left_ref
  32.1 2.0 %collective-permute-done.2.refs_3_ = bf16[128,1024]{1,0:T(8,128)(2,1)S(1)} collective-permute-done((bf16[128,1024]{1,0:T(8,128)(2,1)S(1)}, bf16[128,1024]{1,0:T(8,128)(2,1)S(1)}, u32[]{:S(2)}, u32[]{:S(2)}) %collective-permute-start.2) | collective-permute-done | bytes 262176 | tf_op jit(solution)/shard_map/ppermute | solution.py:187
  34.1 3.6 %collective-permute-done.5.refs_6_ = bf16[128,1024]{1,0:T(8,128)(2,1)S(1)} collective-permute-done((bf16[128,1024]{1,0:T(8,128)(2,1)S(1)}, bf16[128,1024]{1,0:T(8,128)(2,1)S(1)}, u32[]{:S(2)}, u32[]{:S(2)}) %collective-permute-start.5) | collective-permute-done | bytes 262176 | tf_op jit(solution)/shard_map/ppermute | solution.py:187
  37.6 0.0 copy-done.2
  37.6 0.0 copy-done.5
  37.6 0.0 copy-done.6
  37.6 0.0 copy-done.7
  37.6 0.0 copy-done.8
  37.6 0.0 copy-done.3
  37.7 0.0 copy-done.9
  37.7 0.0 copy-start.10
  37.7 0.7 copy-done.10
  38.4 16.4 %fold.1 = f32[32,4096]{1,0:T(8,128)} custom-call(s32[2]{0:T(128)} %pad_add_fusion.ids_ref, s32[1,32]{1,0:T(1,128)} %lengths_ref.1, s32[2,256,1024]{2,1,0:T(8,128)} %signs_ref.1, bf16[4,256,128]{2,1,0:T(8,128)(2,1)} %copy-done.3, bf16[128,1024]{1,0:T(8,128)(2,1)} %copy-done.2, bf16[128,1024]{1,0:T(8,128)(2,1)} %copy-done.5, bf16[128,1024]{1,0:T(8,128)(2,1)} %copy-done.7, ...), custom_call_target="tpu_custom_call" | custom-call | tf_op jit(solution)/shard_map/fold/pallas_call | solution.py:82
  54.8 17.0 %all_to_all.45 = f32[4,8,4096]{2,1,0:T(8,128)} all-to-all(f32[4,8,4096]{2,1,0:T(8,128)} %bitcast.22), channel_id=1, replica_groups=mesh['parts'=2,'blk'=4,'dp'=2,'sub'=2] {'blk'}, dimensions={0} | all-to-all | bytes 1048576 | tf_op jit(solution)/shard_map/all_to_all | solution.py:191
  71.7 2.3 %mix.1 = bf16[32,4096]{1,0:T(8,128)(2,1)} custom-call(f32[32,4096]{1,0:T(8,128)} %bitcast.23), custom_call_target="tpu_custom_call" | custom-call | tf_op jit(solution)/shard_map/mix/pallas_call | solution.py:141
  74.0 11.4 %all_to_all.46 = bf16[4,8,4096]{2,1,0:T(8,128)(2,1)S(1)} all-to-all(bf16[4,8,4096]{2,1,0:T(8,128)(2,1)} %bitcast.26), channel_id=1, replica_groups=mesh['parts'=2,'blk'=4,'dp'=2,'sub'=2] {'blk'}, dimensions={0} | all-to-all | bytes 524288 | tf_op jit(solution)/shard_map/all_to_all | solution.py:191
  85.4 0.0 collective-permute-start.6
  85.4 0.7 copy-done.1
  86.1 10.1 %project.2 = bf16[32,2048]{1,0:T(8,128)(2,1)} custom-call(s32[1]{0:T(128)} %bitcast.ids_ref, bf16[32,4096]{1,0:T(8,128)(2,1)} %bitcast.25, bf16[2,4096,2048]{2,1,0:T(8,128)(2,1)} %bitcast.20), custom_call_target="tpu_custom_call" | custom-call | flops 536870912 | bytes 16777216 | tf_op jit(solution)/shard_map/project/pallas_call | solution.py:166
  96.2 3.3 %all-to-all-start.3 = ((bf16[4,8,2048]{2,1,0:T(8,128)(2,1)}), bf16[4,8,2048]{2,1,0:T(8,128)(2,1)S(1)}, u32[]{:S(2)}, u32[]{:S(2)}) async-start(bf16[4,8,2048]{2,1,0:T(8,128)(2,1)} %bitcast.28), calls=%async_computation.3 | async-start | bytes 262144 | tf_op jit(solution)/shard_map/all_to_all | solution.py:191
  99.5 0.0 collective-permute-done.6.kept_ref
  99.5 0.0 copy-start.4
  99.5 0.7 copy-done.4
  100.2 10.1 %project.3 = bf16[32,2048]{1,0:T(8,128)(2,1)} custom-call(s32[1]{0:T(128)S(6)} %sub.3.ids_ref, bf16[32,4096]{1,0:T(8,128)(2,1)} %copy-done.4, bf16[2,4096,2048]{2,1,0:T(8,128)(2,1)} %bitcast.21), custom_call_target="tpu_custom_call" | custom-call | flops 536870912 | bytes 16777216 | tf_op jit(solution)/shard_map/project/pallas_call | solution.py:166
  110.3 0.0 all-to-all-done.3
  110.3 5.0 %all-to-all-start.4 = ((bf16[4,8,2048]{2,1,0:T(8,128)(2,1)}), bf16[4,8,2048]{2,1,0:T(8,128)(2,1)S(1)}, u32[]{:S(2)}, u32[]{:S(2)}) async-start(bf16[4,8,2048]{2,1,0:T(8,128)(2,1)} %bitcast.27), calls=%async_computation.4 | async-start | bytes 262144 | tf_op jit(solution)/shard_map/all_to_all | solution.py:191
  115.4 5.9 %all-to-all-done.4 = bf16[4,8,2048]{2,1,0:T(8,128)(2,1)S(1)} async-done(((bf16[4,8,2048]{2,1,0:T(8,128)(2,1)}), bf16[4,8,2048]{2,1,0:T(8,128)(2,1)S(1)}, u32[]{:S(2)}, u32[]{:S(2)}) %all-to-all-start.4) | async-done | bytes 131104 | tf_op jit(solution)/shard_map/all_to_all | solution.py:191
  121.4 0.1 copy.8
  121.5 0.8 maximum_bitcast_fusion
  (10 shorter events, 0.1 us)
Async XLA Ops:
  0.0 1.0 copy-start
  1.1 36.6 %copy-start.2 = (bf16[128,1024]{1,0:T(8,128)(2,1)}, bf16[128,1024]{1,0:T(8,128)(2,1)S(1)}, u32[]{:S(2)}) copy-start(bf16[128,1024]{1,0:T(8,128)(2,1)S(1)} %dynamic-slice_bitcast_fusion.refs_0_) | copy-start | bytes 786436
  1.1 10.5 %collective-permute-start = (bf16[128,1024]{1,0:T(8,128)(2,1)S(1)}, bf16[128,1024]{1,0:T(8,128)(2,1)S(1)}, u32[]{:S(2)}, u32[]{:S(2)}) collective-permute-start(bf16[128,1024]{1,0:T(8,128)(2,1)S(1)} %dynamic-slice_bitcast_fusion.refs_0_), channel_id=1, source_target_pairs={{0,4},{4,8},{8,12},{1,5},{5,9},{9,13},{2,6},{6,10},{10,14},{3,7},{... | collective-permute-start | bytes 786440 | tf_op jit(solution)/shard_map/ppermute | solution.py:187
  6.1 9.9 %collective-permute-start.3 = (bf16[128,1024]{1,0:T(8,128)(2,1)S(1)}, bf16[128,1024]{1,0:T(8,128)(2,1)S(1)}, u32[]{:S(2)}, u32[]{:S(2)}) collective-permute-start(bf16[128,1024]{1,0:T(8,128)(2,1)S(1)} %dynamic-slice_bitcast_fusion.refs_0_), channel_id=1, source_target_pairs={{4,0},{8,4},{12,8},{5,1},{9,5},{13,9},{6,2},{10,6},{14,10},{7,3},{... | collective-permute-start | bytes 786440 | tf_op jit(solution)/shard_map/ppermute | solution.py:187
  11.6 26.0 %copy-start.5 = (bf16[128,1024]{1,0:T(8,128)(2,1)}, bf16[128,1024]{1,0:T(8,128)(2,1)S(1)}, u32[]{:S(2)}) copy-start(bf16[128,1024]{1,0:T(8,128)(2,1)S(1)} %collective-permute-done.refs_1_) | copy-start | bytes 786436
  11.6 13.5 %collective-permute-start.1 = (bf16[128,1024]{1,0:T(8,128)(2,1)S(1)}, bf16[128,1024]{1,0:T(8,128)(2,1)S(1)}, u32[]{:S(2)}, u32[]{:S(2)}) collective-permute-start(bf16[128,1024]{1,0:T(8,128)(2,1)S(1)} %collective-permute-done.refs_1_), channel_id=1, source_target_pairs={{0,4},{4,8},{8,12},{1,5},{5,9},{9,13},{2,6},{6,10},{10,14},{3,7},{... | collective-permute-start | bytes 786440 | tf_op jit(solution)/shard_map/ppermute | solution.py:187
  16.0 21.6 %copy-start.6 = (bf16[128,1024]{1,0:T(8,128)(2,1)}, bf16[128,1024]{1,0:T(8,128)(2,1)S(1)}, u32[]{:S(2)}) copy-start(bf16[128,1024]{1,0:T(8,128)(2,1)S(1)} %collective-permute-done.3.refs_4_) | copy-start | bytes 786436
  16.0 13.0 %collective-permute-start.4 = (bf16[128,1024]{1,0:T(8,128)(2,1)S(1)}, bf16[128,1024]{1,0:T(8,128)(2,1)S(1)}, u32[]{:S(2)}, u32[]{:S(2)}) collective-permute-start(bf16[128,1024]{1,0:T(8,128)(2,1)S(1)} %collective-permute-done.3.refs_4_), channel_id=1, source_target_pairs={{4,0},{8,4},{12,8},{5,1},{9,5},{13,9},{6,2},{10,6},{14,10},{7,3},{... | collective-permute-start | bytes 786440 | tf_op jit(solution)/shard_map/ppermute | solution.py:187
  19.1 13.0 %all-to-all-start = ((bf16[4,256,128]{2,1,0:T(8,128)(2,1)}), bf16[4,256,128]{2,1,0:T(8,128)(2,1)S(1)}, u32[]{:S(2)}, u32[]{:S(2)}) async-start(bf16[4,256,128]{2,1,0:T(8,128)(2,1)} %bitcast.4), calls=%async_computation | async-start | bytes 524288 | tf_op jit(solution)/shard_map/all_to_all | solution.py:191
  25.1 12.6 %copy-start.7 = (bf16[128,1024]{1,0:T(8,128)(2,1)}, bf16[128,1024]{1,0:T(8,128)(2,1)S(1)}, u32[]{:S(2)}) copy-start(bf16[128,1024]{1,0:T(8,128)(2,1)S(1)} %collective-permute-done.1.refs_2_) | copy-start | bytes 786436
  25.1 9.0 %collective-permute-start.2 = (bf16[128,1024]{1,0:T(8,128)(2,1)S(1)}, bf16[128,1024]{1,0:T(8,128)(2,1)S(1)}, u32[]{:S(2)}, u32[]{:S(2)}) collective-permute-start(bf16[128,1024]{1,0:T(8,128)(2,1)S(1)} %collective-permute-done.1.refs_2_), channel_id=1, source_target_pairs={{0,4},{4,8},{8,12},{1,5},{5,9},{9,13},{2,6},{6,10},{10,14},{3,7},{... | collective-permute-start | bytes 786440 | tf_op jit(solution)/shard_map/ppermute | solution.py:187
  29.0 8.6 %copy-start.8 = (bf16[128,1024]{1,0:T(8,128)(2,1)}, bf16[128,1024]{1,0:T(8,128)(2,1)S(1)}, u32[]{:S(2)}) copy-start(bf16[128,1024]{1,0:T(8,128)(2,1)S(1)} %collective-permute-done.4.refs_5_) | copy-start | bytes 786436
  29.0 8.6 %collective-permute-start.5 = (bf16[128,1024]{1,0:T(8,128)(2,1)S(1)}, bf16[128,1024]{1,0:T(8,128)(2,1)S(1)}, u32[]{:S(2)}, u32[]{:S(2)}) collective-permute-start(bf16[128,1024]{1,0:T(8,128)(2,1)S(1)} %collective-permute-done.4.refs_5_), channel_id=1, source_target_pairs={{4,0},{8,4},{12,8},{5,1},{9,5},{13,9},{6,2},{10,6},{14,10},{7,3},{... | collective-permute-start | bytes 786440 | tf_op jit(solution)/shard_map/ppermute | solution.py:187
  32.1 5.6 %copy-start.3 = (bf16[4,256,128]{2,1,0:T(8,128)(2,1)}, bf16[4,256,128]{2,1,0:T(8,128)(2,1)S(1)}, u32[]{:S(2)}) copy-start(bf16[4,256,128]{2,1,0:T(8,128)(2,1)S(1)} %all-to-all-done.left_ref) | copy-start | bytes 786436
  34.1 3.6 %copy-start.9 = (bf16[128,1024]{1,0:T(8,128)(2,1)}, bf16[128,1024]{1,0:T(8,128)(2,1)S(1)}, u32[]{:S(2)}) copy-start(bf16[128,1024]{1,0:T(8,128)(2,1)S(1)} %collective-permute-done.2.refs_3_) | copy-start | bytes 786436
  37.7 0.7 copy-start.10
  85.4 0.7 copy-start.1
  85.4 14.1 %collective-permute-start.6 = (bf16[32,4096]{1,0:T(8,128)(2,1)S(1)}, bf16[32,4096]{1,0:T(8,128)(2,1)S(1)}, u32[]{:S(2)}, u32[]{:S(2)}) collective-permute-start(bf16[32,4096]{1,0:T(8,128)(2,1)S(1)} %bitcast.24), channel_id=1, source_target_pairs={{0,1},{1,0},{2,3},{3,2},{4,5},{5,4},{6,7},{7,6},{8,9},{9,8},{10,11... | collective-permute-start | bytes 786440 | tf_op jit(solution)/shard_map/ppermute | solution.py:219
  96.2 14.1 %all-to-all-start.3 = ((bf16[4,8,2048]{2,1,0:T(8,128)(2,1)}), bf16[4,8,2048]{2,1,0:T(8,128)(2,1)S(1)}, u32[]{:S(2)}, u32[]{:S(2)}) async-start(bf16[4,8,2048]{2,1,0:T(8,128)(2,1)} %bitcast.28), calls=%async_computation.3 | async-start | bytes 262144 | tf_op jit(solution)/shard_map/all_to_all | solution.py:191
  99.5 0.7 copy-start.4
  110.3 11.0 %all-to-all-start.4 = ((bf16[4,8,2048]{2,1,0:T(8,128)(2,1)}), bf16[4,8,2048]{2,1,0:T(8,128)(2,1)S(1)}, u32[]{:S(2)}, u32[]{:S(2)}) async-start(bf16[4,8,2048]{2,1,0:T(8,128)(2,1)} %bitcast.27), calls=%async_computation.4 | async-start | bytes 262144 | tf_op jit(solution)/shard_map/all_to_all | solution.py:191

commit v2 on v1

v2 whole, which is shorter than its diff:
```python
import functools
import math

import jax
import jax.numpy as jnp
from jax import lax
from jax.experimental import pallas as pl
from jax.experimental.pallas import tpu as pltpu
from jax.sharding import PartitionSpec as P


F32 = jnp.float32
BF16 = jnp.bfloat16
NT = (((1,), (1,)), ((), ()))
FINE = 4
SMEM_SPEC = pl.BlockSpec(memory_space=pltpu.SMEM)
VMEM_SPEC = pl.BlockSpec(memory_space=pltpu.VMEM)
HBM_SPEC = pl.BlockSpec(memory_space=pltpu.HBM)


def params(mib):
    return pltpu.CompilerParams(vmem_limit_bytes=mib << 20)


def iota(shape, dim):
    return lax.broadcasted_iota(jnp.int32, shape, dim)


def parity_sign(values):
    for shift in (8, 4, 2, 1):
        values = jnp.bitwise_xor(values, jnp.right_shift(values, shift))
    return (1 - 2 * jnp.bitwise_and(values, 1)).astype(F32)


def split_bf16(x):
    hi = x.astype(BF16)
    return hi, (x - hi.astype(F32)).astype(BF16)


def prepare_kernel(kept, ids_ref, signs_ref, spread_ref, order_ref):
    _, width = signs_ref.shape[1:]
    coarse = kept // FINE
    part = width // coarse
    source = iota((width, width), 0)
    place = (source // FINE) % coarse * part + source // kept * FINE + source % FINE
    order_ref[...] = jnp.where(place == iota((width, width), 1), 1.0, 0.0).astype(BF16)
    signed = (2 * signs_ref[ids_ref[0]] - 1).astype(F32).astype(BF16)
    for c in range(coarse):
        cols = slice(c * part, (c + 1) * part)
        piece = jnp.dot(signed, order_ref[:, cols], preferred_element_type=F32)
        for f in range(FINE):
            spread_ref[c, f] = jnp.where(iota(piece.shape, 1) % FINE == f, piece, 0.0).astype(BF16)


def prepare(ids, signs, kept):
    rows, width = signs.shape[1:]
    coarse = kept // FINE
    return pl.pallas_call(
        functools.partial(prepare_kernel, kept),
        in_specs=[SMEM_SPEC, VMEM_SPEC],
        out_specs=[VMEM_SPEC, VMEM_SPEC],
        out_shape=[
            jax.ShapeDtypeStruct((coarse, FINE, rows, width // coarse), BF16),
            jax.ShapeDtypeStruct((width, width), BF16),
        ],
        name="prepare",
        compiler_params=params(8),
        cost_estimate=pl.CostEstimate(flops=16_000_000, bytes_accessed=8 * rows * width, transcendentals=0),
    )(ids, signs)


def fetch_kernel(pick, ids_ref, weights_ref, out_ref, sems):
    layer = ids_ref[0] if pick == 0 else 1 - ids_ref[0]
    count = sems.shape[0]
    part = out_ref.shape[0] // count
    copies = [
        pltpu.make_async_copy(
            weights_ref.at[layer, pl.ds(i * part, part)], out_ref.at[pl.ds(i * part, part)], sems.at[i]
        )
        for i in range(count)
    ]
    for copy in copies:
        copy.start()
    for copy in copies:
        copy.wait()


def fetch(ids, weights, pick):
    depth, width = weights.shape[1:]
    return pl.pallas_call(
        functools.partial(fetch_kernel, pick),
        in_specs=[SMEM_SPEC, HBM_SPEC],
        out_specs=VMEM_SPEC,
        out_shape=jax.ShapeDtypeStruct((depth, width), BF16),
        scratch_shapes=[pltpu.SemaphoreType.DMA((4,))],
        name="fetch",
        compiler_params=params(24 if pick == 0 else 4),
        cost_estimate=pl.CostEstimate(flops=16_000_000, bytes_accessed=2 * depth * width, transcendentals=0),
    )(ids, weights)


def fold_kernel(blocks, kept, tile, ids_ref, lengths_ref, spread_ref, order_ref, left_ref, own_ref, *refs):
    mine_refs, theirs_refs = refs[:blocks - 1], refs[blocks - 1:2 * blocks - 2]
    out_ref, b_scr, a_scr, hot_scr = refs[2 * blocks - 2:]
    tokens, width = b_scr.shape
    tok_local = tokens // blocks
    documents = hot_scr.shape[0]
    coarse = kept // FINE
    part = width // coarse
    half, me = ids_ref[0], ids_ref[1]

    @pl.when(pl.program_id(0) == 0)
    def _():
        def place(value, block):
            rows = pl.ds(pl.multiple_of(block * tok_local, tok_local), tok_local)
            b_scr[rows, :] = jnp.dot(value[...], order_ref[...], preferred_element_type=F32).astype(BF16)

        place(own_ref.at[half], me)
        for step in range(1, blocks):
            toward = jnp.where(half == 0, step, -step)
            for value, block in (
                (mine_refs[step - 1].at[half], me - toward),
                (theirs_refs[step - 1].at[half], me + toward),
            ):
                pl.when((block >= 0) & (block < blocks))(functools.partial(place, value, block))
        for block in range(blocks):
            a_scr[:, block * tok_local:(block + 1) * tok_local] = left_ref[block].astype(F32)
        square = (documents, documents)
        spread = jnp.broadcast_to(lengths_ref[...].astype(F32), square)
        ends = jnp.sum(jnp.where(iota(square, 1) <= iota(square, 0), spread, 0.0), axis=1, keepdims=True)
        starts = jnp.sum(jnp.where(iota(square, 1) < iota(square, 0), spread, 0.0), axis=1, keepdims=True)
        token = iota((documents, tokens), 1).astype(F32)
        hot = jnp.where((token >= starts) & (token < ends), 1.0, 0.0).astype(BF16)
        hot_scr[:, :tokens] = hot
        hot_scr[:, tokens:] = hot

    row0 = pl.multiple_of(pl.program_id(0) * tile, tile)
    left = a_scr[pl.ds(row0, tile), :]
    terms = []
    for c in range(coarse):
        signed = spread_ref[c, :, pl.ds(row0, tile), :].reshape(FINE * tile, part)
        mixed = lax.dot_general(signed, b_scr[:, c * part:(c + 1) * part], NT, preferred_element_type=F32)
        mixed = (mixed.reshape(FINE, tile, tokens) * left[None]).reshape(FINE * tile, tokens)
        terms.append(split_bf16(mixed))
    for u in range(tile // 16):
        pieces = [
            jnp.concatenate(
                [terms[c][w][f * tile + u * 16:f * tile + (u + 1) * 16] for c in range(coarse) for f in range(FINE)],
                axis=0,
            )
            for w in range(2)
        ]
        out_ref[:, u * 16 * kept:(u + 1) * 16 * kept] = lax.dot_general(
            hot_scr[...], jnp.concatenate(pieces, axis=1), NT, preferred_element_type=F32
        )


def fold(ids, lengths, spread, order, left, own, mine, theirs, kept):
    blocks, rows_block, tok_local = left.shape
    width = own.shape[2]
    tokens = blocks * tok_local
    documents = lengths.shape[1]
    tile = min(64, rows_block)
    return pl.pallas_call(
        functools.partial(fold_kernel, blocks, kept, tile),
        grid=(rows_block // tile,),
        in_specs=[SMEM_SPEC] + [VMEM_SPEC] * (5 + 2 * (blocks - 1)),
        out_specs=pl.BlockSpec((documents, tile * kept), lambda g: (0, g)),
        scratch_shapes=[
            pltpu.VMEM((tokens, width), BF16),
            pltpu.VMEM((rows_block, tokens), F32),
            pltpu.VMEM((documents, 2 * tokens), BF16),
        ],
        out_shape=jax.ShapeDtypeStruct((documents, rows_block * kept), F32),
        name="fold",
        compiler_params=params(16),
        cost_estimate=pl.CostEstimate(flops=32_000_000, bytes_accessed=1 << 20, transcendentals=0),
    )(ids, lengths, spread, order, left, own, *mine, *theirs)


def mix_kernel(blocks, kept, scale, in_ref, out_ref):
    rows, lanes = in_ref.shape
    docs = rows // blocks
    tile = 16 * kept
    count = lanes // tile
    row, col = iota((tile, tile), 0), iota((tile, tile), 1)
    over_rows = jnp.bitwise_and(row % 16, col // kept)
    over_cols = jnp.bitwise_and(row // 16, col % kept)
    table = (parity_sign(over_rows) * parity_sign(over_cols)).astype(BF16)
    stacked = jnp.concatenate([in_ref[:, t * tile:(t + 1) * tile] for t in range(count)], axis=0)
    hi, lo = split_bf16(stacked)
    both = jnp.dot(jnp.concatenate([hi, lo], axis=0), table, preferred_element_type=F32)
    both = both[:count * rows] + both[count * rows:]
    parts = [[both[t * rows + b * docs:t * rows + (b + 1) * docs] for b in range(blocks)] for t in range(count)]

    def butterfly(items):
        step = 1
        while step < len(items):
            for low in range(len(items)):
                if not low & step:
                    a, b = items[low], items[low | step]
                    items[low], items[low | step] = a + b, a - b
            step *= 2
        return items

    for b in range(blocks):
        column = butterfly([parts[t][b] for t in range(count)])
        for t in range(count):
            parts[t][b] = column[t]
    for t in range(count):
        done = butterfly(parts[t])
        for b in range(blocks):
            out_ref[b * docs:(b + 1) * docs, t * tile:(t + 1) * tile] = (done[b] * scale).astype(BF16)


def mix(folded, blocks, kept, scale):
    return pl.pallas_call(
        functools.partial(mix_kernel, blocks, kept, scale),
        in_specs=[VMEM_SPEC],
        out_specs=VMEM_SPEC,
        out_shape=jax.ShapeDtypeStruct(folded.shape, BF16),
        name="mix",
        compiler_params=params(8),
    )(folded)


def project_kernel(ids_ref, kept_ref, other_ref, first_ref, second_ref, out_ref):
    _, width = first_ref.shape
    part = min(512, width)
    for order, (rows_ref, weights_ref) in enumerate(((kept_ref, first_ref), (other_ref, second_ref))):
        layer = ids_ref[0] if order == 0 else 1 - ids_ref[0]

        @pl.loop(0, width // part)
        def _(step):
            col = pl.multiple_of(step * part, part)
            out_ref[:, pl.ds(pl.multiple_of(layer * width + col, 128), part)] = jnp.dot(
                rows_ref[...], weights_ref[:, pl.ds(col, part)], preferred_element_type=F32
            ).astype(out_ref.dtype)


def project(ids, kept, other, first, second):
    documents, depth = kept.shape
    width = first.shape[1]
    return pl.pallas_call(
        project_kernel,
        in_specs=[SMEM_SPEC] + [VMEM_SPEC] * 4,
        out_specs=VMEM_SPEC,
        out_shape=jax.ShapeDtypeStruct((documents, 2 * width), BF16),
        name="project",
        compiler_params=params(8),
        cost_estimate=pl.CostEstimate(
            flops=4 * documents * depth * width, bytes_accessed=4 * depth * width, transcendentals=0
        ),
    )(ids, kept, other, first, second)


def exchange(rows):
    return lax.all_to_all(rows, "blk", split_axis=0, concat_axis=0, tiled=True)


def shards(in_factors, out_factors, lengths, signs, projection):
    blocks = lax.axis_size("blk")
    halves = lax.axis_size("sub")
    my_block = lax.axis_index("blk")
    my_half = lax.axis_index("sub")
    layers, _, tok_local, in_width = in_factors.shape
    out_width = out_factors.shape[3]
    assert layers == halves == 2
    rows_block = in_width // blocks
    documents = lengths.shape[1]
    docs = documents // blocks
    kept_cols = projection.shape[2]
    scale = 1.0 / math.sqrt(in_width * out_width)
    ids = jnp.stack([my_half, my_block]).astype(jnp.int32)
    weights = projection.reshape(layers, rows_block * kept_cols, projection.shape[3])

    routes = [(2 * b, 2 * b + 2) for b in range(blocks - 1)] + [(2 * b + 3, 2 * b + 1) for b in range(blocks - 1)]
    own = out_factors[:, 0]
    mine, theirs = [], []
    for _ in range(1, blocks):
        got = lax.ppermute(mine[-1] if mine else own, ("blk", "sub"), routes)
        mine.append(got)
        theirs.append(lax.ppermute(got, "sub", [(0, 1), (1, 0)]))
    left = lax.dynamic_index_in_dim(in_factors[:, 0], my_half, 0, keepdims=False)
    left = exchange(left.T.reshape(blocks, rows_block, tok_local))
    spread, order = prepare(ids, signs, kept_cols)
    first = fetch(ids, weights, 0)
    second = fetch(ids, weights, 1)
    folded = exchange(fold(ids, lengths, spread, order, left, own, mine, theirs, kept_cols))
    kept = exchange(mix(folded, blocks, kept_cols, scale))
    other = lax.ppermute(kept, "sub", [(0, 1), (1, 0)])
    terms = exchange(project(ids, kept, other, first, second))
    terms = terms.reshape(blocks, docs, layers, weights.shape[2]).astype(F32)
    return jnp.sum(terms, axis=0)[None]


def solution(mesh):
    return jax.shard_map(
        shards,
        mesh=mesh,
        in_specs=(
            P(None, ("parts", "dp"), "blk", None),
            P(None, ("parts", "dp"), "blk", None),
            P(("parts", "dp"), None),
            P(None, "blk", None),
            P(None, "blk", None, "sub"),
        ),
        out_specs=P(("parts", "dp"), "blk", None, "sub"),
        check_vma=False,
    )
```

time: 124 us -> 129 us (1.040); the launches traced: 122 us -> 129 us
  local copies, waits for them, and re-layouts: 5.06 us -> 18.4 us
  Pallas kernels: 38.9 us -> 25.8 us
  blocking collectives: 28.4 us -> 39.5 us
  starting transfers between devices: 31.5 us -> 21 us
  waiting for transfers between devices: 16.9 us -> 23.8 us
  other arithmetic: 1.45 us -> 0.11 us
    unnamed x22 -> x16, local copies, waits for them, and re-layouts: 3.13 us -> 16.8 us
    pallas_call x4 -> x6, Pallas kernels: 38.9 us -> 25.8 us  [the longest x2 8.13 us: fetch(): pl.pallas_call(functools.partial(fetch_kernel, pick), in_specs=[SMEM_SPEC...]
    all_to_all x2 -> x3, blocking collectives: 28.4 us -> 39.5 us  [exchange(): return lax.all_to_all(rows, 'blk', split_axis=0, concat_axis=0, tiled=True)]
    ppermute x6, waiting for transfers between devices: 9.75 us -> 19 us  [the longest x3 19 us: shards(): got = lax.ppermute(mine[-1] if mine else own, ('blk', 'sub'), routes)]
    all_to_all x3 -> x1, starting transfers between devices: 14.3 us -> 5.88 us  [exchange(): return lax.all_to_all(rows, 'blk', split_axis=0, concat_axis=0, tiled=True)]
    all_to_all x3 -> x1, waiting for transfers between devices: 7.12 us -> 4.8 us  [exchange(): return lax.all_to_all(rows, 'blk', split_axis=0, concat_axis=0, tiled=True)]
    ppermute x6, starting transfers between devices: 17.2 us -> 15.1 us  [the longest x3 14.6 us: shards(): got = lax.ppermute(mine[-1] if mine else own, ('blk', 'sub'), routes)]
  transfers between devices with their start and end apart: 10 -> 8, of which waited for: 5 -> 4; matrix products, arithmetic and copies ran while one was open for 2% -> 1% of each run, Pallas kernels for 17% -> 8%
where the time goes in v2:
time: 129 us
  blocking collectives  39.5 us (31%)
  Pallas kernels  25.8 us (20%)
  waiting for transfers between devices  23.8 us (18%)
  starting transfers between devices  21 us (16%)
  local copies, waits for them, and re-layouts  18.4 us (14%)
    all_to_all x3, blocking collectives, exchange(): return lax.all_to_all(rows, 'blk', split_axis=0, concat_axis=0, tiled=True)  39.5 us
    ppermute x3, waiting for transfers between devices, shards(): got = lax.ppermute(mine[-1] if mine else own, ('blk', 'sub'), routes)  19 us
    unnamed x16, local copies, waits for them, and re-layouts  16.8 us
    ppermute x3, starting transfers between devices, shards(): got = lax.ppermute(mine[-1] if mine else own, ('blk', 'sub'), routes)  14.6 us
    pallas_call x2, Pallas kernels, fetch(): pl.pallas_call(functools.partial(fetch_kernel, pick), in_specs=[SMEM_SPEC...  8.13 us
    pallas_call x1, Pallas kernels, fold(): pl.pallas_call(functools.partial(fold_kernel, blocks, kept, tile), grid=(...  8.07 us
    pallas_call x1, Pallas kernels, project(): pl.pallas_call(project_kernel, in_specs=[SMEM_SPEC] + [VMEM_SPEC] * 4, ou...  7.27 us
    all_to_all x1, starting transfers between devices, exchange(): return lax.all_to_all(rows, 'blk', split_axis=0, concat_axis=0, tiled=True)  5.88 us
  transfers between devices with their start and end apart: 8, of which 4 were waited for; matrix products, arithmetic and copies ran while one was open for 1% of the time, Pallas kernels for 8%

profile of v2, /device:TPU:0, one launch (start us, length us, event | category | flops | bytes accessed | tf_op | source)
XLA Modules:
  0.0 128.7 jit_solution(16930420668686089475)
XLA Ops:
  0.0 0.0 copy-start
  0.0 5.1 %collective-permute-start = (bf16[2,128,1024]{2,1,0:T(8,128)(2,1)}, bf16[2,128,1024]{2,1,0:T(8,128)(2,1)S(1)}, u32[]{:S(2)}, u32[]{:S(2)}) collective-permute-start(bf16[2,128,1024]{2,1,0:T(8,128)(2,1)} %bitcast.22), channel_id=1, source_target_pairs={{0,4},{4,8},{8,12},{5,1},{9,5},{13,9},{2,6},{6,10},{10,14},{7,3},{... | collective-permute-start | bytes 1572872 | tf_op jit(solution)/shard_map/ppermute | solution.py:281
  5.1 7.0 %collective-permute-done.refs_0_ = bf16[2,128,1024]{2,1,0:T(8,128)(2,1)S(1)} collective-permute-done((bf16[2,128,1024]{2,1,0:T(8,128)(2,1)}, bf16[2,128,1024]{2,1,0:T(8,128)(2,1)S(1)}, u32[]{:S(2)}, u32[]{:S(2)}) %collective-permute-start) | collective-permute-done | bytes 524320 | tf_op jit(solution)/shard_map/ppermute | solution.py:281
  12.1 4.3 %collective-permute-start.1 = (bf16[2,128,1024]{2,1,0:T(8,128)(2,1)S(1)}, bf16[2,128,1024]{2,1,0:T(8,128)(2,1)S(1)}, u32[]{:S(2)}, u32[]{:S(2)}) collective-permute-start(bf16[2,128,1024]{2,1,0:T(8,128)(2,1)S(1)} %collective-permute-done.refs_0_), channel_id=1, source_target_pairs={{0,4},{4,8},{8,12},{5,1},{9,5},{13,9},{2,6},{6,10},{10,14},{7,3},{... | collective-permute-start | bytes 1572872 | tf_op jit(solution)/shard_map/ppermute | solution.py:281
  16.4 6.6 %collective-permute-done.1.refs_1_ = bf16[2,128,1024]{2,1,0:T(8,128)(2,1)S(1)} collective-permute-done((bf16[2,128,1024]{2,1,0:T(8,128)(2,1)S(1)}, bf16[2,128,1024]{2,1,0:T(8,128)(2,1)S(1)}, u32[]{:S(2)}, u32[]{:S(2)}) %collective-permute-start.1) | collective-permute-done | bytes 524320 | tf_op jit(solution)/shard_map/ppermute | solution.py:281
  23.0 5.2 %collective-permute-start.2 = (bf16[2,128,1024]{2,1,0:T(8,128)(2,1)S(1)}, bf16[2,128,1024]{2,1,0:T(8,128)(2,1)}, u32[]{:S(2)}, u32[]{:S(2)}) collective-permute-start(bf16[2,128,1024]{2,1,0:T(8,128)(2,1)S(1)} %collective-permute-done.1.refs_1_), channel_id=1, source_target_pairs={{0,4},{4,8},{8,12},{5,1},{9,5},{13,9},{2,6},{6,10},{10,14},{7,3},{... | collective-permute-start | bytes 1572872 | tf_op jit(solution)/shard_map/ppermute | solution.py:281
  28.2 0.0 collective-permute-start.3
  28.2 0.5 collective-permute-start.4
  28.7 5.4 %collective-permute-done.2.refs_2_ = bf16[2,128,1024]{2,1,0:T(8,128)(2,1)} collective-permute-done((bf16[2,128,1024]{2,1,0:T(8,128)(2,1)S(1)}, bf16[2,128,1024]{2,1,0:T(8,128)(2,1)}, u32[]{:S(2)}, u32[]{:S(2)}) %collective-permute-start.2) | collective-permute-done | bytes 524320 | tf_op jit(solution)/shard_map/ppermute | solution.py:281
  34.1 0.0 collective-permute-start.5
  34.1 0.0 copy-done
  34.1 0.8 copy.6
  35.0 5.9 %all-to-all-start = ((bf16[4,256,128]{2,1,0:T(8,128)(2,1)}), bf16[4,256,128]{2,1,0:T(8,128)(2,1)S(1)}, u32[]{:S(2)}, u32[]{:S(2)}) async-start(bf16[4,256,128]{2,1,0:T(8,128)(2,1)} %bitcast.4), calls=%async_computation | async-start | bytes 524288 | tf_op jit(solution)/shard_map/all_to_all | solution.py:258
  40.9 0.1 pad_add_fusion.ids_ref
  40.9 0.0 copy-start.5
  40.9 1.6 %copy-done.5 = s32[2,256,1024]{2,1,0:T(8,128)S(1)} copy-done((s32[2,256,1024]{2,1,0:T(8,128)S(1)}, s32[2,256,1024]{2,1,0:T(8,128)}, u32[]{:S(2)}) %copy-start.5) | copy-done | bytes 2097176
  42.5 1.7 %prepare.1 = (bf16[4,4,256,256]{3,2,1,0:T(8,128)(2,1)S(1)}, bf16[1024,1024]{1,0:T(8,128)(2,1)S(1)}) custom-call(s32[2]{0:T(128)S(1)} %pad_add_fusion.ids_ref, s32[2,256,1024]{2,1,0:T(8,128)S(1)} %copy-done.5), custom_call_target="tpu_custom_call" | custom-call | flops 16000000 | bytes 2097152 | tf_op jit(solution)/shard_map/prepare/pallas_call | solution.py:58
  44.3 0.0 copy-start.3
  44.3 1.3 %copy-done.3 = bf16[1024,1024]{1,0:T(8,128)(2,1)} copy-done((bf16[1024,1024]{1,0:T(8,128)(2,1)}, bf16[1024,1024]{1,0:T(8,128)(2,1)S(1)}, u32[]{:S(2)}) %copy-start.3) | copy-done | bytes 2097176
  45.6 4.8 %all-to-all-done.left_ref = bf16[4,256,128]{2,1,0:T(8,128)(2,1)S(1)} async-done(((bf16[4,256,128]{2,1,0:T(8,128)(2,1)}), bf16[4,256,128]{2,1,0:T(8,128)(2,1)S(1)}, u32[]{:S(2)}, u32[]{:S(2)}) %all-to-all-start) | async-done | bytes 262176 | tf_op jit(solution)/shard_map/all_to_all | solution.py:258
  50.4 0.0 collective-permute-done.3.refs_3_
  50.4 0.0 collective-permute-done.4.refs_4_
  50.4 0.0 collective-permute-done.5.refs_5_
  50.4 0.0 copy-start.4
  50.4 1.6 %copy-done.4 = bf16[1024,1024]{1,0:T(8,128)(2,1)S(1)} copy-done((bf16[1024,1024]{1,0:T(8,128)(2,1)S(1)}, bf16[1024,1024]{1,0:T(8,128)(2,1)}, u32[]{:S(2)}) %copy-start.4) | copy-done | bytes 2097176
  52.0 0.0 copy-start.6
  52.0 1.0 copy-done.6
  53.0 0.0 copy-start.7
  53.1 0.7 copy-done.7
  53.7 8.1 %fold.1 = f32[32,4096]{1,0:T(8,128)S(1)} custom-call(s32[2]{0:T(128)S(1)} %pad_add_fusion.ids_ref, s32[1,32]{1,0:T(1,128)S(1)} %copy-done.7, bf16[4,4,256,256]{3,2,1,0:T(8,128)(2,1)S(1)} %get-tuple-element.7.spread_ref, bf16[1024,1024]{1,0:T(8,128)(2,1)S(1)} %copy-done.4, bf16[4,256,128]{2,1,0:T(8,128)(2,1)S(1)} %all-to-all-done.left_ref, ...), custom_call_target="tpu_custom_call" | custom-call | flops 32000000 | bytes 1048576 | tf_op jit(solution)/shard_map/fold/pallas_call | solution.py:164
  61.8 16.3 %all_to_all.36 = f32[4,8,4096]{2,1,0:T(8,128)S(1)} all-to-all(f32[4,8,4096]{2,1,0:T(8,128)S(1)} %bitcast.16), channel_id=1, replica_groups=mesh['parts'=2,'blk'=4,'dp'=2,'sub'=2] {'blk'}, dimensions={0} | all-to-all | bytes 1048576 | tf_op jit(solution)/shard_map/all_to_all | solution.py:258
  78.1 0.6 mix.1
  78.7 11.0 %all_to_all.37 = bf16[4,8,4096]{2,1,0:T(8,128)(2,1)S(1)} all-to-all(bf16[4,8,4096]{2,1,0:T(8,128)(2,1)S(1)} %bitcast.21), channel_id=1, replica_groups=mesh['parts'=2,'blk'=4,'dp'=2,'sub'=2] {'blk'}, dimensions={0} | all-to-all | bytes 524288 | tf_op jit(solution)/shard_map/all_to_all | solution.py:258
  89.7 0.0 collective-permute-start.6
  89.7 0.0 copy-start.2
  89.7 10.5 %copy-done.2 = bf16[2,256,16,2048]{3,2,1,0:T(8,128)(2,1)S(1)} copy-done((bf16[2,256,16,2048]{3,2,1,0:T(8,128)(2,1)S(1)}, bf16[2,256,16,2048]{3,2,1,0:T(8,128)(2,1)}, u32[]{:S(2)}) %copy-start.2) | copy-done | bytes 33554456
  100.2 1.7 %fetch.3.second_ref = bf16[4096,2048]{1,0:T(8,128)(2,1)S(1)} custom-call(s32[2]{0:T(128)S(1)} %pad_add_fusion.ids_ref, bf16[2,4096,2048]{2,1,0:T(8,128)(2,1)S(1)} %bitcast.15), custom_call_target="tpu_custom_call" | custom-call | flops 16000000 | bytes 16777216 | tf_op jit(solution)/shard_map/fetch/pallas_call | solution.py:90
  101.9 0.0 copy-start.1
  101.9 6.4 %fetch.2.first_ref = bf16[4096,2048]{1,0:T(8,128)(2,1)S(1)} custom-call(s32[2]{0:T(128)S(1)} %pad_add_fusion.ids_ref, bf16[2,4096,2048]{2,1,0:T(8,128)(2,1)} %bitcast.14), custom_call_target="tpu_custom_call" | custom-call | flops 16000000 | bytes 16777216 | tf_op jit(solution)/shard_map/fetch/pallas_call | solution.py:90
  108.4 0.0 collective-permute-done.6.other_ref
  108.4 7.3 %project.1 = bf16[32,4096]{1,0:T(8,128)(2,1)S(1)} custom-call(s32[2]{0:T(128)S(1)} %pad_add_fusion.ids_ref, bf16[32,4096]{1,0:T(8,128)(2,1)S(1)} %bitcast.19, bf16[32,4096]{1,0:T(8,128)(2,1)S(1)} %collective-permute-done.6.other_ref, bf16[4096,2048]{1,0:T(8,128)(2,1)S(1)} %fetch.2.first_ref, bf16[4096,2048]{1,0:T(8,128)(2,1)S(1)} %fetch.3.second_ref), custom_call_target="tpu_custom_call" | custom-call | flops 1073741824 | bytes 33554432 | tf_op jit(solution)/shard_map/project/pallas_call | solution.py:244
  115.7 12.2 %all_to_all.38 = bf16[4,8,4096]{2,1,0:T(8,128)(2,1)S(1)} all-to-all(bf16[4,8,4096]{2,1,0:T(8,128)(2,1)S(1)} %bitcast.20), channel_id=1, replica_groups=mesh['parts'=2,'blk'=4,'dp'=2,'sub'=2] {'blk'}, dimensions={0} | all-to-all | bytes 524288 | tf_op jit(solution)/shard_map/all_to_all | solution.py:258
  127.9 0.8 broadcast_in_dim.3
  128.7 0.0 copy-done.1
  (2 shorter events, 0.1 us)
Async XLA Ops:
  0.0 34.1 %copy-start = (bf16[2,1,128,1024]{3,2,1,0:T(8,128)(2,1)S(1)}, bf16[2,1,128,1024]{3,2,1,0:T(8,128)(2,1)}, u32[]{:S(2)}) copy-start(bf16[2,1,128,1024]{3,2,1,0:T(8,128)(2,1)} %param.5) | copy-start | bytes 1572868
  0.0 12.1 %collective-permute-start = (bf16[2,128,1024]{2,1,0:T(8,128)(2,1)}, bf16[2,128,1024]{2,1,0:T(8,128)(2,1)S(1)}, u32[]{:S(2)}, u32[]{:S(2)}) collective-permute-start(bf16[2,128,1024]{2,1,0:T(8,128)(2,1)} %bitcast.22), channel_id=1, source_target_pairs={{0,4},{4,8},{8,12},{5,1},{9,5},{13,9},{2,6},{6,10},{10,14},{7,3},{... | collective-permute-start | bytes 1572872 | tf_op jit(solution)/shard_map/ppermute | solution.py:281
  12.1 11.0 %collective-permute-start.1 = (bf16[2,128,1024]{2,1,0:T(8,128)(2,1)S(1)}, bf16[2,128,1024]{2,1,0:T(8,128)(2,1)S(1)}, u32[]{:S(2)}, u32[]{:S(2)}) collective-permute-start(bf16[2,128,1024]{2,1,0:T(8,128)(2,1)S(1)} %collective-permute-done.refs_0_), channel_id=1, source_target_pairs={{0,4},{4,8},{8,12},{5,1},{9,5},{13,9},{2,6},{6,10},{10,14},{7,3},{... | collective-permute-start | bytes 1572872 | tf_op jit(solution)/shard_map/ppermute | solution.py:281
  23.0 11.1 %collective-permute-start.2 = (bf16[2,128,1024]{2,1,0:T(8,128)(2,1)S(1)}, bf16[2,128,1024]{2,1,0:T(8,128)(2,1)}, u32[]{:S(2)}, u32[]{:S(2)}) collective-permute-start(bf16[2,128,1024]{2,1,0:T(8,128)(2,1)S(1)} %collective-permute-done.1.refs_1_), channel_id=1, source_target_pairs={{0,4},{4,8},{8,12},{5,1},{9,5},{13,9},{2,6},{6,10},{10,14},{7,3},{... | collective-permute-start | bytes 1572872 | tf_op jit(solution)/shard_map/ppermute | solution.py:281
  28.2 22.2 %collective-permute-start.3 = (bf16[2,128,1024]{2,1,0:T(8,128)(2,1)S(1)}, bf16[2,128,1024]{2,1,0:T(8,128)(2,1)}, u32[]{:S(2)}, u32[]{:S(2)}) collective-permute-start(bf16[2,128,1024]{2,1,0:T(8,128)(2,1)S(1)} %collective-permute-done.refs_0_), channel_id=1, source_target_pairs={{0,1},{1,0},{2,3},{3,2},{4,5},{5,4},{6,7},{7,6},{8,9},{9,8},{10,11... | collective-permute-start | bytes 1572872 | tf_op jit(solution)/shard_map/ppermute | solution.py:283
  28.2 22.2 %collective-permute-start.4 = (bf16[2,128,1024]{2,1,0:T(8,128)(2,1)S(1)}, bf16[2,128,1024]{2,1,0:T(8,128)(2,1)}, u32[]{:S(2)}, u32[]{:S(2)}) collective-permute-start(bf16[2,128,1024]{2,1,0:T(8,128)(2,1)S(1)} %collective-permute-done.1.refs_1_), channel_id=1, source_target_pairs={{0,1},{1,0},{2,3},{3,2},{4,5},{5,4},{6,7},{7,6},{8,9},{9,8},{10,11... | collective-permute-start | bytes 1572872 | tf_op jit(solution)/shard_map/ppermute | solution.py:283
  34.1 16.3 %collective-permute-start.5 = (bf16[2,128,1024]{2,1,0:T(8,128)(2,1)}, bf16[2,128,1024]{2,1,0:T(8,128)(2,1)}, u32[]{:S(2)}, u32[]{:S(2)}) collective-permute-start(bf16[2,128,1024]{2,1,0:T(8,128)(2,1)} %collective-permute-done.2.refs_2_), channel_id=1, source_target_pairs={{0,1},{1,0},{2,3},{3,2},{4,5},{5,4},{6,7},{7,6},{8,9},{9,8},{10,11... | collective-permute-start | bytes 1572872 | tf_op jit(solution)/shard_map/ppermute | solution.py:283
  35.0 15.4 %all-to-all-start = ((bf16[4,256,128]{2,1,0:T(8,128)(2,1)}), bf16[4,256,128]{2,1,0:T(8,128)(2,1)S(1)}, u32[]{:S(2)}, u32[]{:S(2)}) async-start(bf16[4,256,128]{2,1,0:T(8,128)(2,1)} %bitcast.4), calls=%async_computation | async-start | bytes 524288 | tf_op jit(solution)/shard_map/all_to_all | solution.py:258
  40.9 1.6 %copy-start.5 = (s32[2,256,1024]{2,1,0:T(8,128)S(1)}, s32[2,256,1024]{2,1,0:T(8,128)}, u32[]{:S(2)}) copy-start(s32[2,256,1024]{2,1,0:T(8,128)} %signs_ref.1) | copy-start | bytes 6291460
  44.3 1.3 %copy-start.3 = (bf16[1024,1024]{1,0:T(8,128)(2,1)}, bf16[1024,1024]{1,0:T(8,128)(2,1)S(1)}, u32[]{:S(2)}) copy-start(bf16[1024,1024]{1,0:T(8,128)(2,1)S(1)} %get-tuple-element.8.order_ref) | copy-start | bytes 6291460
  50.4 1.6 %copy-start.4 = (bf16[1024,1024]{1,0:T(8,128)(2,1)S(1)}, bf16[1024,1024]{1,0:T(8,128)(2,1)}, u32[]{:S(2)}) copy-start(bf16[1024,1024]{1,0:T(8,128)(2,1)} %copy-done.3) | copy-start | bytes 6291460
  52.0 1.0 copy-start.6
  53.0 0.7 copy-start.7
  89.7 18.7 %collective-permute-start.6 = (bf16[32,4096]{1,0:T(8,128)(2,1)S(1)}, bf16[32,4096]{1,0:T(8,128)(2,1)S(1)}, u32[]{:S(2)}, u32[]{:S(2)}) collective-permute-start(bf16[32,4096]{1,0:T(8,128)(2,1)S(1)} %bitcast.18), channel_id=1, source_target_pairs={{0,1},{1,0},{2,3},{3,2},{4,5},{5,4},{6,7},{7,6},{8,9},{9,8},{10,11... | collective-permute-start | bytes 786440 | tf_op jit(solution)/shard_map/ppermute | solution.py:291
  89.7 10.5 %copy-start.2 = (bf16[2,256,16,2048]{3,2,1,0:T(8,128)(2,1)S(1)}, bf16[2,256,16,2048]{3,2,1,0:T(8,128)(2,1)}, u32[]{:S(2)}) copy-start(bf16[2,256,16,2048]{3,2,1,0:T(8,128)(2,1)} %param.9) | copy-start | bytes 100663296
  101.9 26.8 %copy-start.1 = (bf16[2,1,128,1024]{3,2,1,0:T(8,128)(2,1)S(1)}, bf16[2,1,128,1024]{3,2,1,0:T(8,128)(2,1)}, u32[]{:S(2)}) copy-start(bf16[2,1,128,1024]{3,2,1,0:T(8,128)(2,1)} %param.5) | copy-start | bytes 1572868

commit v3 on v2

--- a/solution.py
+++ b/solution.py
@@ -64,7 +64,7 @@
             jax.ShapeDtypeStruct((width, width), BF16),
         ],
         name="prepare",
-        compiler_params=params(8),
+        compiler_params=params(3),
         cost_estimate=pl.CostEstimate(flops=16_000_000, bytes_accessed=8 * rows * width, transcendentals=0),
     )(ids, signs)
 
@@ -94,7 +94,7 @@
         out_shape=jax.ShapeDtypeStruct((depth, width), BF16),
         scratch_shapes=[pltpu.SemaphoreType.DMA((4,))],
         name="fetch",
-        compiler_params=params(24 if pick == 0 else 4),
+        compiler_params=params(22 if pick == 0 else 16),
         cost_estimate=pl.CostEstimate(flops=16_000_000, bytes_accessed=2 * depth * width, transcendentals=0),
     )(ids, weights)
 
@@ -173,7 +173,7 @@
         ],
         out_shape=jax.ShapeDtypeStruct((documents, rows_block * kept), F32),
         name="fold",
-        compiler_params=params(16),
+        compiler_params=params(8),
         cost_estimate=pl.CostEstimate(flops=32_000_000, bytes_accessed=1 << 20, transcendentals=0),
     )(ids, lengths, spread, order, left, own, *mine, *theirs)
 
@@ -220,7 +220,7 @@
         out_specs=VMEM_SPEC,
         out_shape=jax.ShapeDtypeStruct(folded.shape, BF16),
         name="mix",
-        compiler_params=params(8),
+        compiler_params=params(2),
     )(folded)
 
 
@@ -247,7 +247,7 @@
         out_specs=VMEM_SPEC,
         out_shape=jax.ShapeDtypeStruct((documents, 2 * width), BF16),
         name="project",
-        compiler_params=params(8),
+        compiler_params=params(2),
         cost_estimate=pl.CostEstimate(
             flops=4 * documents * depth * width, bytes_accessed=4 * depth * width, transcendentals=0
         ),

time: 129 us -> 135 us (1.047)
  Pallas kernels: 25.8 us -> 30.6 us
    pallas_call x2, Pallas kernels: 8.13 us -> 12.9 us  [fetch(): pl.pallas_call(functools.partial(fetch_kernel, pick), in_specs=[SMEM_SPEC...]
    unnamed x16 -> x18, local copies, waits for them, and re-layouts: 16.8 us -> 17.7 us
  transfers between devices with their start and end apart: 8 -> 8, of which waited for: 4 -> 4; matrix products, arithmetic and copies ran while one was open for 1% -> 1% of each run, Pallas kernels for 8% -> 11%
where the time goes in v3:
time: 135 us; the launch traced here: 134 us
  blocking collectives  39.5 us (29%)
  Pallas kernels  30.6 us (23%)
  waiting for transfers between devices  23.8 us (18%)
  starting transfers between devices  21 us (16%)
  local copies, waits for them, and re-layouts  19.3 us (14%)
    all_to_all x3, blocking collectives, exchange(): return lax.all_to_all(rows, 'blk', split_axis=0, concat_axis=0, tiled=True)  39.5 us
    ppermute x3, waiting for transfers between devices, shards(): got = lax.ppermute(mine[-1] if mine else own, ('blk', 'sub'), routes)  19 us
    unnamed x18, local copies, waits for them, and re-layouts  17.7 us
    ppermute x3, starting transfers between devices, shards(): got = lax.ppermute(mine[-1] if mine else own, ('blk', 'sub'), routes)  14.6 us
    pallas_call x2, Pallas kernels, fetch(): pl.pallas_call(functools.partial(fetch_kernel, pick), in_specs=[SMEM_SPEC...  12.9 us
    pallas_call x1, Pallas kernels, fold(): pl.pallas_call(functools.partial(fold_kernel, blocks, kept, tile), grid=(...  8.07 us
    pallas_call x1, Pallas kernels, project(): pl.pallas_call(project_kernel, in_specs=[SMEM_SPEC] + [VMEM_SPEC] * 4, ou...  7.27 us
    all_to_all x1, starting transfers between devices, exchange(): return lax.all_to_all(rows, 'blk', split_axis=0, concat_axis=0, tiled=True)  5.88 us
  transfers between devices with their start and end apart: 8, of which 4 were waited for; matrix products, arithmetic and copies ran while one was open for 1% of the time, Pallas kernels for 11%

profile of v3, /device:TPU:0, one launch (start us, length us, event | category | flops | bytes accessed | tf_op | source)
XLA Modules:
  0.0 134.4 jit_solution(944031113014101084)
XLA Ops:
  0.0 0.0 copy-start
  0.0 5.1 %collective-permute-start = (bf16[2,128,1024]{2,1,0:T(8,128)(2,1)}, bf16[2,128,1024]{2,1,0:T(8,128)(2,1)S(1)}, u32[]{:S(2)}, u32[]{:S(2)}) collective-permute-start(bf16[2,128,1024]{2,1,0:T(8,128)(2,1)} %bitcast.20), channel_id=1, source_target_pairs={{0,4},{4,8},{8,12},{5,1},{9,5},{13,9},{2,6},{6,10},{10,14},{7,3},{... | collective-permute-start | bytes 1572872 | tf_op jit(solution)/shard_map/ppermute | solution.py:281
  5.1 7.0 %collective-permute-done.refs_0_ = bf16[2,128,1024]{2,1,0:T(8,128)(2,1)S(1)} collective-permute-done((bf16[2,128,1024]{2,1,0:T(8,128)(2,1)}, bf16[2,128,1024]{2,1,0:T(8,128)(2,1)S(1)}, u32[]{:S(2)}, u32[]{:S(2)}) %collective-permute-start) | collective-permute-done | bytes 524320 | tf_op jit(solution)/shard_map/ppermute | solution.py:281
  12.1 4.3 %collective-permute-start.1 = (bf16[2,128,1024]{2,1,0:T(8,128)(2,1)S(1)}, bf16[2,128,1024]{2,1,0:T(8,128)(2,1)S(1)}, u32[]{:S(2)}, u32[]{:S(2)}) collective-permute-start(bf16[2,128,1024]{2,1,0:T(8,128)(2,1)S(1)} %collective-permute-done.refs_0_), channel_id=1, source_target_pairs={{0,4},{4,8},{8,12},{5,1},{9,5},{13,9},{2,6},{6,10},{10,14},{7,3},{... | collective-permute-start | bytes 1572872 | tf_op jit(solution)/shard_map/ppermute | solution.py:281
  16.4 6.6 %collective-permute-done.1.refs_1_ = bf16[2,128,1024]{2,1,0:T(8,128)(2,1)S(1)} collective-permute-done((bf16[2,128,1024]{2,1,0:T(8,128)(2,1)S(1)}, bf16[2,128,1024]{2,1,0:T(8,128)(2,1)S(1)}, u32[]{:S(2)}, u32[]{:S(2)}) %collective-permute-start.1) | collective-permute-done | bytes 524320 | tf_op jit(solution)/shard_map/ppermute | solution.py:281
  23.0 5.2 %collective-permute-start.2 = (bf16[2,128,1024]{2,1,0:T(8,128)(2,1)S(1)}, bf16[2,128,1024]{2,1,0:T(8,128)(2,1)}, u32[]{:S(2)}, u32[]{:S(2)}) collective-permute-start(bf16[2,128,1024]{2,1,0:T(8,128)(2,1)S(1)} %collective-permute-done.1.refs_1_), channel_id=1, source_target_pairs={{0,4},{4,8},{8,12},{5,1},{9,5},{13,9},{2,6},{6,10},{10,14},{7,3},{... | collective-permute-start | bytes 1572872 | tf_op jit(solution)/shard_map/ppermute | solution.py:281
  28.2 0.0 collective-permute-start.3
  28.2 0.5 collective-permute-start.4
  28.8 5.4 %collective-permute-done.2.refs_2_ = bf16[2,128,1024]{2,1,0:T(8,128)(2,1)} collective-permute-done((bf16[2,128,1024]{2,1,0:T(8,128)(2,1)S(1)}, bf16[2,128,1024]{2,1,0:T(8,128)(2,1)}, u32[]{:S(2)}, u32[]{:S(2)}) %collective-permute-start.2) | collective-permute-done | bytes 524320 | tf_op jit(solution)/shard_map/ppermute | solution.py:281
  34.1 0.0 collective-permute-start.5
  34.1 0.0 copy-done
  34.1 0.8 copy.6
  35.0 5.9 %all-to-all-start = ((bf16[4,256,128]{2,1,0:T(8,128)(2,1)}), bf16[4,256,128]{2,1,0:T(8,128)(2,1)S(1)}, u32[]{:S(2)}, u32[]{:S(2)}) async-start(bf16[4,256,128]{2,1,0:T(8,128)(2,1)} %bitcast.4), calls=%async_computation | async-start | bytes 524288 | tf_op jit(solution)/shard_map/all_to_all | solution.py:258
  40.9 0.1 pad_add_fusion.ids_ref
  40.9 0.0 copy-start.6
  40.9 1.6 %copy-done.6 = s32[2,256,1024]{2,1,0:T(8,128)S(1)} copy-done((s32[2,256,1024]{2,1,0:T(8,128)S(1)}, s32[2,256,1024]{2,1,0:T(8,128)}, u32[]{:S(2)}) %copy-start.6) | copy-done | bytes 2097176
  42.5 1.7 %prepare.1 = (bf16[4,4,256,256]{3,2,1,0:T(8,128)(2,1)S(1)}, bf16[1024,1024]{1,0:T(8,128)(2,1)S(1)}) custom-call(s32[2]{0:T(128)S(1)} %pad_add_fusion.ids_ref, s32[2,256,1024]{2,1,0:T(8,128)S(1)} %copy-done.6), custom_call_target="tpu_custom_call" | custom-call | flops 16000000 | bytes 2097152 | tf_op jit(solution)/shard_map/prepare/pallas_call | solution.py:58
  44.3 0.0 copy-start.4
  44.3 1.3 copy-done.4
  45.6 4.8 %all-to-all-done.left_ref = bf16[4,256,128]{2,1,0:T(8,128)(2,1)S(1)} async-done(((bf16[4,256,128]{2,1,0:T(8,128)(2,1)}), bf16[4,256,128]{2,1,0:T(8,128)(2,1)S(1)}, u32[]{:S(2)}, u32[]{:S(2)}) %all-to-all-start) | async-done | bytes 262176 | tf_op jit(solution)/shard_map/all_to_all | solution.py:258
  50.4 0.0 collective-permute-done.3.refs_3_
  50.4 0.0 collective-permute-done.4.refs_4_
  50.4 0.0 collective-permute-done.5.refs_5_
  50.4 0.0 copy-start.5
  50.4 1.6 %copy-done.5 = bf16[1024,1024]{1,0:T(8,128)(2,1)S(1)} copy-done((bf16[1024,1024]{1,0:T(8,128)(2,1)S(1)}, bf16[1024,1024]{1,0:T(8,128)(2,1)}, u32[]{:S(2)}) %copy-start.5) | copy-done | bytes 2097176
  52.0 0.0 copy-start.7
  52.0 1.0 copy-done.7
  53.0 0.0 copy-start.8
  53.1 0.7 copy-done.8
  53.7 8.1 %fold.1 = f32[32,4096]{1,0:T(8,128)S(1)} custom-call(s32[2]{0:T(128)S(1)} %pad_add_fusion.ids_ref, s32[1,32]{1,0:T(1,128)S(1)} %copy-done.8, bf16[4,4,256,256]{3,2,1,0:T(8,128)(2,1)S(1)} %get-tuple-element.7.spread_ref, bf16[1024,1024]{1,0:T(8,128)(2,1)S(1)} %copy-done.5, bf16[4,256,128]{2,1,0:T(8,128)(2,1)S(1)} %all-to-all-done.left_ref, ...), custom_call_target="tpu_custom_call" | custom-call | flops 32000000 | bytes 1048576 | tf_op jit(solution)/shard_map/fold/pallas_call | solution.py:164
  61.8 16.3 %all_to_all.36 = f32[4,8,4096]{2,1,0:T(8,128)S(1)} all-to-all(f32[4,8,4096]{2,1,0:T(8,128)S(1)} %bitcast.14), channel_id=1, replica_groups=mesh['parts'=2,'blk'=4,'dp'=2,'sub'=2] {'blk'}, dimensions={0} | all-to-all | bytes 1048576 | tf_op jit(solution)/shard_map/all_to_all | solution.py:258
  78.1 0.6 mix.1
  78.7 11.0 %all_to_all.37 = bf16[4,8,4096]{2,1,0:T(8,128)(2,1)S(1)} all-to-all(bf16[4,8,4096]{2,1,0:T(8,128)(2,1)S(1)} %bitcast.19), channel_id=1, replica_groups=mesh['parts'=2,'blk'=4,'dp'=2,'sub'=2] {'blk'}, dimensions={0} | all-to-all | bytes 524288 | tf_op jit(solution)/shard_map/all_to_all | solution.py:258
  89.7 0.0 collective-permute-start.6
  89.7 6.4 %fetch.3.second_ref = bf16[4096,2048]{1,0:T(8,128)(2,1)S(1)} custom-call(s32[2]{0:T(128)S(1)} %pad_add_fusion.ids_ref, bf16[2,4096,2048]{2,1,0:T(8,128)(2,1)} %bitcast.22), custom_call_target="tpu_custom_call" | custom-call | flops 16000000 | bytes 16777216 | tf_op jit(solution)/shard_map/fetch/pallas_call | solution.py:90
  96.1 0.0 copy-start.1
  96.1 6.4 %fetch.2.first_ref = bf16[4096,2048]{1,0:T(8,128)(2,1)S(1)} custom-call(s32[2]{0:T(128)S(1)} %pad_add_fusion.ids_ref, bf16[2,4096,2048]{2,1,0:T(8,128)(2,1)} %bitcast.23), custom_call_target="tpu_custom_call" | custom-call | flops 16000000 | bytes 16777216 | tf_op jit(solution)/shard_map/fetch/pallas_call | solution.py:90
  102.6 0.0 copy-start.2
  102.6 5.7 %copy-done.2 = bf16[4096,2048]{1,0:T(8,128)(2,1)} copy-done((bf16[4096,2048]{1,0:T(8,128)(2,1)}, bf16[4096,2048]{1,0:T(8,128)(2,1)S(1)}, u32[]{:S(2)}) %copy-start.2) | copy-done | bytes 16777240
  108.3 0.0 collective-permute-done.6.other_ref
  108.3 0.0 copy-start.3
  108.3 5.8 %copy-done.3 = bf16[4096,2048]{1,0:T(8,128)(2,1)S(1)} copy-done((bf16[4096,2048]{1,0:T(8,128)(2,1)S(1)}, bf16[4096,2048]{1,0:T(8,128)(2,1)}, u32[]{:S(2)}) %copy-start.3) | copy-done | bytes 16777240
  114.1 7.3 %project.1 = bf16[32,4096]{1,0:T(8,128)(2,1)S(1)} custom-call(s32[2]{0:T(128)S(1)} %pad_add_fusion.ids_ref, bf16[32,4096]{1,0:T(8,128)(2,1)S(1)} %bitcast.17, bf16[32,4096]{1,0:T(8,128)(2,1)S(1)} %collective-permute-done.6.other_ref, bf16[4096,2048]{1,0:T(8,128)(2,1)S(1)} %copy-done.3, bf16[4096,2048]{1,0:T(8,128)(2,1)S(1)} %fetch.3.second_ref), custom_call_target="tpu_custom_call" | custom-call | flops 1073741824 | bytes 33554432 | tf_op jit(solution)/shard_map/project/pallas_call | solution.py:244
  121.4 12.2 %all_to_all.38 = bf16[4,8,4096]{2,1,0:T(8,128)(2,1)S(1)} all-to-all(bf16[4,8,4096]{2,1,0:T(8,128)(2,1)S(1)} %bitcast.18), channel_id=1, replica_groups=mesh['parts'=2,'blk'=4,'dp'=2,'sub'=2] {'blk'}, dimensions={0} | all-to-all | bytes 524288 | tf_op jit(solution)/shard_map/all_to_all | solution.py:258
  133.6 0.8 broadcast_in_dim.3
  134.4 0.0 copy-done.1
  (2 shorter events, 0.1 us)
Async XLA Ops:
  0.0 34.1 %copy-start = (bf16[2,1,128,1024]{3,2,1,0:T(8,128)(2,1)S(1)}, bf16[2,1,128,1024]{3,2,1,0:T(8,128)(2,1)}, u32[]{:S(2)}) copy-start(bf16[2,1,128,1024]{3,2,1,0:T(8,128)(2,1)} %param.5) | copy-start | bytes 1572868
  0.0 12.1 %collective-permute-start = (bf16[2,128,1024]{2,1,0:T(8,128)(2,1)}, bf16[2,128,1024]{2,1,0:T(8,128)(2,1)S(1)}, u32[]{:S(2)}, u32[]{:S(2)}) collective-permute-start(bf16[2,128,1024]{2,1,0:T(8,128)(2,1)} %bitcast.20), channel_id=1, source_target_pairs={{0,4},{4,8},{8,12},{5,1},{9,5},{13,9},{2,6},{6,10},{10,14},{7,3},{... | collective-permute-start | bytes 1572872 | tf_op jit(solution)/shard_map/ppermute | solution.py:281
  12.1 11.0 %collective-permute-start.1 = (bf16[2,128,1024]{2,1,0:T(8,128)(2,1)S(1)}, bf16[2,128,1024]{2,1,0:T(8,128)(2,1)S(1)}, u32[]{:S(2)}, u32[]{:S(2)}) collective-permute-start(bf16[2,128,1024]{2,1,0:T(8,128)(2,1)S(1)} %collective-permute-done.refs_0_), channel_id=1, source_target_pairs={{0,4},{4,8},{8,12},{5,1},{9,5},{13,9},{2,6},{6,10},{10,14},{7,3},{... | collective-permute-start | bytes 1572872 | tf_op jit(solution)/shard_map/ppermute | solution.py:281
  23.0 11.1 %collective-permute-start.2 = (bf16[2,128,1024]{2,1,0:T(8,128)(2,1)S(1)}, bf16[2,128,1024]{2,1,0:T(8,128)(2,1)}, u32[]{:S(2)}, u32[]{:S(2)}) collective-permute-start(bf16[2,128,1024]{2,1,0:T(8,128)(2,1)S(1)} %collective-permute-done.1.refs_1_), channel_id=1, source_target_pairs={{0,4},{4,8},{8,12},{5,1},{9,5},{13,9},{2,6},{6,10},{10,14},{7,3},{... | collective-permute-start | bytes 1572872 | tf_op jit(solution)/shard_map/ppermute | solution.py:281
  28.2 22.2 %collective-permute-start.3 = (bf16[2,128,1024]{2,1,0:T(8,128)(2,1)S(1)}, bf16[2,128,1024]{2,1,0:T(8,128)(2,1)}, u32[]{:S(2)}, u32[]{:S(2)}) collective-permute-start(bf16[2,128,1024]{2,1,0:T(8,128)(2,1)S(1)} %collective-permute-done.refs_0_), channel_id=1, source_target_pairs={{0,1},{1,0},{2,3},{3,2},{4,5},{5,4},{6,7},{7,6},{8,9},{9,8},{10,11... | collective-permute-start | bytes 1572872 | tf_op jit(solution)/shard_map/ppermute | solution.py:283
  28.2 22.2 %collective-permute-start.4 = (bf16[2,128,1024]{2,1,0:T(8,128)(2,1)S(1)}, bf16[2,128,1024]{2,1,0:T(8,128)(2,1)}, u32[]{:S(2)}, u32[]{:S(2)}) collective-permute-start(bf16[2,128,1024]{2,1,0:T(8,128)(2,1)S(1)} %collective-permute-done.1.refs_1_), channel_id=1, source_target_pairs={{0,1},{1,0},{2,3},{3,2},{4,5},{5,4},{6,7},{7,6},{8,9},{9,8},{10,11... | collective-permute-start | bytes 1572872 | tf_op jit(solution)/shard_map/ppermute | solution.py:283
  34.1 16.3 %collective-permute-start.5 = (bf16[2,128,1024]{2,1,0:T(8,128)(2,1)}, bf16[2,128,1024]{2,1,0:T(8,128)(2,1)}, u32[]{:S(2)}, u32[]{:S(2)}) collective-permute-start(bf16[2,128,1024]{2,1,0:T(8,128)(2,1)} %collective-permute-done.2.refs_2_), channel_id=1, source_target_pairs={{0,1},{1,0},{2,3},{3,2},{4,5},{5,4},{6,7},{7,6},{8,9},{9,8},{10,11... | collective-permute-start | bytes 1572872 | tf_op jit(solution)/shard_map/ppermute | solution.py:283
  35.0 15.4 %all-to-all-start = ((bf16[4,256,128]{2,1,0:T(8,128)(2,1)}), bf16[4,256,128]{2,1,0:T(8,128)(2,1)S(1)}, u32[]{:S(2)}, u32[]{:S(2)}) async-start(bf16[4,256,128]{2,1,0:T(8,128)(2,1)} %bitcast.4), calls=%async_computation | async-start | bytes 524288 | tf_op jit(solution)/shard_map/all_to_all | solution.py:258
  40.9 1.6 %copy-start.6 = (s32[2,256,1024]{2,1,0:T(8,128)S(1)}, s32[2,256,1024]{2,1,0:T(8,128)}, u32[]{:S(2)}) copy-start(s32[2,256,1024]{2,1,0:T(8,128)} %signs_ref.1) | copy-start | bytes 6291460
  44.3 1.3 copy-start.4
  50.4 1.6 %copy-start.5 = (bf16[1024,1024]{1,0:T(8,128)(2,1)S(1)}, bf16[1024,1024]{1,0:T(8,128)(2,1)}, u32[]{:S(2)}) copy-start(bf16[1024,1024]{1,0:T(8,128)(2,1)} %copy-done.4) | copy-start | bytes 6291460
  52.0 1.0 copy-start.7
  53.0 0.7 copy-start.8
  89.7 18.6 %collective-permute-start.6 = (bf16[32,4096]{1,0:T(8,128)(2,1)S(1)}, bf16[32,4096]{1,0:T(8,128)(2,1)S(1)}, u32[]{:S(2)}, u32[]{:S(2)}) collective-permute-start(bf16[32,4096]{1,0:T(8,128)(2,1)S(1)} %bitcast.16), channel_id=1, source_target_pairs={{0,1},{1,0},{2,3},{3,2},{4,5},{5,4},{6,7},{7,6},{8,9},{9,8},{10,11... | collective-permute-start | bytes 786440 | tf_op jit(solution)/shard_map/ppermute | solution.py:291
  96.1 38.3 %copy-start.1 = (bf16[2,1,128,1024]{3,2,1,0:T(8,128)(2,1)S(1)}, bf16[2,1,128,1024]{3,2,1,0:T(8,128)(2,1)}, u32[]{:S(2)}) copy-start(bf16[2,1,128,1024]{3,2,1,0:T(8,128)(2,1)} %param.5) | copy-start | bytes 1572868
  102.6 5.7 %copy-start.2 = (bf16[4096,2048]{1,0:T(8,128)(2,1)}, bf16[4096,2048]{1,0:T(8,128)(2,1)S(1)}, u32[]{:S(2)}) copy-start(bf16[4096,2048]{1,0:T(8,128)(2,1)S(1)} %fetch.2.first_ref) | copy-start | bytes 50331652
  108.3 5.8 %copy-start.3 = (bf16[4096,2048]{1,0:T(8,128)(2,1)S(1)}, bf16[4096,2048]{1,0:T(8,128)(2,1)}, u32[]{:S(2)}) copy-start(bf16[4096,2048]{1,0:T(8,128)(2,1)} %copy-done.2) | copy-start | bytes 50331652

commit v4 on v3

--- a/solution.py
+++ b/solution.py
@@ -69,67 +69,47 @@
     )(ids, signs)
 
 
-def fetch_kernel(pick, ids_ref, weights_ref, out_ref, sems):
-    layer = ids_ref[0] if pick == 0 else 1 - ids_ref[0]
-    count = sems.shape[0]
-    part = out_ref.shape[0] // count
-    copies = [
-        pltpu.make_async_copy(
-            weights_ref.at[layer, pl.ds(i * part, part)], out_ref.at[pl.ds(i * part, part)], sems.at[i]
-        )
-        for i in range(count)
-    ]
-    for copy in copies:
-        copy.start()
-    for copy in copies:
-        copy.wait()
-
-
-def fetch(ids, weights, pick):
-    depth, width = weights.shape[1:]
-    return pl.pallas_call(
-        functools.partial(fetch_kernel, pick),
-        in_specs=[SMEM_SPEC, HBM_SPEC],
-        out_specs=VMEM_SPEC,
-        out_shape=jax.ShapeDtypeStruct((depth, width), BF16),
-        scratch_shapes=[pltpu.SemaphoreType.DMA((4,))],
-        name="fetch",
-        compiler_params=params(22 if pick == 0 else 16),
-        cost_estimate=pl.CostEstimate(flops=16_000_000, bytes_accessed=2 * depth * width, transcendentals=0),
-    )(ids, weights)
-
-
-def fold_kernel(blocks, kept, tile, ids_ref, lengths_ref, spread_ref, order_ref, left_ref, own_ref, *refs):
-    mine_refs, theirs_refs = refs[:blocks - 1], refs[blocks - 1:2 * blocks - 2]
-    out_ref, b_scr, a_scr, hot_scr = refs[2 * blocks - 2:]
+def fold_kernel(kept, tile, masks, last, *refs):
+    ids_ref, lengths_ref, spread_ref, order_ref, left_ref, more_ref, *refs = refs
+    right_refs = refs[:len(masks)]
+    if last:
+        out_ref, b_scr, a_scr, hot_scr = refs[len(masks):]
+    else:
+        out_ref, first_ref, b_scr, a_scr, hot_scr, sems = refs[len(masks):]
     tokens, width = b_scr.shape
-    tok_local = tokens // blocks
+    tok_local = tokens // len(masks)
     documents = hot_scr.shape[0]
     coarse = kept // FINE
     part = width // coarse
     half, me = ids_ref[0], ids_ref[1]
 
+    def copies():
+        count = sems.shape[0]
+        rows = first_ref.shape[0] // count
+        return [
+            pltpu.make_async_copy(
+                more_ref.at[half, pl.ds(i * rows, rows)], first_ref.at[pl.ds(i * rows, rows)], sems.at[i]
+            )
+            for i in range(count)
+        ]
+
     @pl.when(pl.program_id(0) == 0)
     def _():
-        def place(value, block):
-            rows = pl.ds(pl.multiple_of(block * tok_local, tok_local), tok_local)
-            b_scr[rows, :] = jnp.dot(value[...], order_ref[...], preferred_element_type=F32).astype(BF16)
-
-        place(own_ref.at[half], me)
-        for step in range(1, blocks):
-            toward = jnp.where(half == 0, step, -step)
-            for value, block in (
-                (mine_refs[step - 1].at[half], me - toward),
-                (theirs_refs[step - 1].at[half], me + toward),
-            ):
-                pl.when((block >= 0) & (block < blocks))(functools.partial(place, value, block))
-        for block in range(blocks):
-            a_scr[:, block * tok_local:(block + 1) * tok_local] = left_ref[block].astype(F32)
+        if not last:
+            for copy in copies():
+                copy.start()
+        for at, (mask, right) in enumerate(zip(masks, right_refs)):
+            b_scr[at * tok_local:(at + 1) * tok_local, :] = jnp.dot(
+                right[...], order_ref[...], preferred_element_type=F32
+            ).astype(BF16)
+            a_scr[:, at * tok_local:(at + 1) * tok_local] = left_ref[jnp.bitwise_xor(me, mask)].astype(F32)
         square = (documents, documents)
         spread = jnp.broadcast_to(lengths_ref[...].astype(F32), square)
         ends = jnp.sum(jnp.where(iota(square, 1) <= iota(square, 0), spread, 0.0), axis=1, keepdims=True)
         starts = jnp.sum(jnp.where(iota(square, 1) < iota(square, 0), spread, 0.0), axis=1, keepdims=True)
-        token = iota((documents, tokens), 1).astype(F32)
+        place = iota((documents, tokens), 1)
+        mask = place // tok_local + masks[0]
+        token = (jnp.bitwise_xor(mask, me) * tok_local + place % tok_local).astype(F32)
         hot = jnp.where((token >= starts) & (token < ends), 1.0, 0.0).astype(BF16)
         hot_scr[:, :tokens] = hot
         hot_scr[:, tokens:] = hot
@@ -150,32 +130,44 @@
             )
             for w in range(2)
         ]
-        out_ref[:, u * 16 * kept:(u + 1) * 16 * kept] = lax.dot_general(
+        total = lax.dot_general(
             hot_scr[...], jnp.concatenate(pieces, axis=1), NT, preferred_element_type=F32
         )
-
-
-def fold(ids, lengths, spread, order, left, own, mine, theirs, kept):
-    blocks, rows_block, tok_local = left.shape
-    width = own.shape[2]
-    tokens = blocks * tok_local
+        lanes = slice(u * 16 * kept, (u + 1) * 16 * kept)
+        out_ref[:, lanes] = total + more_ref[:, lanes] if last else total
+
+    if not last:
+        @pl.when(pl.program_id(0) == pl.num_programs(0) - 1)
+        def _():
+            for copy in copies():
+                copy.wait()
+
+
+def fold(ids, lengths, spread, order, left, rights, masks, kept, weights=None, partial=None):
+    _, rows_block, tok_local = left.shape
+    width = order.shape[0]
+    tokens = len(masks) * tok_local
     documents = lengths.shape[1]
     tile = min(64, rows_block)
+    last = weights is None
+    out_spec = pl.BlockSpec((documents, tile * kept), lambda g: (0, g))
+    out_shape = jax.ShapeDtypeStruct((documents, rows_block * kept), F32)
+    scratch = [
+        pltpu.VMEM((tokens, width), BF16),
+        pltpu.VMEM((rows_block, tokens), F32),
+        pltpu.VMEM((documents, 2 * tokens), BF16),
+    ]
     return pl.pallas_call(
-        functools.partial(fold_kernel, blocks, kept, tile),
+        functools.partial(fold_kernel, kept, tile, masks, last),
         grid=(rows_block // tile,),
-        in_specs=[SMEM_SPEC] + [VMEM_SPEC] * (5 + 2 * (blocks - 1)),
-        out_specs=pl.BlockSpec((documents, tile * kept), lambda g: (0, g)),
-        scratch_shapes=[
-            pltpu.VMEM((tokens, width), BF16),
-            pltpu.VMEM((rows_block, tokens), F32),
-            pltpu.VMEM((documents, 2 * tokens), BF16),
-        ],
-        out_shape=jax.ShapeDtypeStruct((documents, rows_block * kept), F32),
-        name="fold",
-        compiler_params=params(8),
+        in_specs=[SMEM_SPEC] + [VMEM_SPEC] * 4 + [out_spec if last else HBM_SPEC] + [VMEM_SPEC] * len(masks),
+        out_specs=out_spec if last else [out_spec, VMEM_SPEC],
+        scratch_shapes=scratch if last else scratch + [pltpu.SemaphoreType.DMA((4,))],
+        out_shape=out_shape if last else [out_shape, jax.ShapeDtypeStruct(weights.shape[1:], BF16)],
+        name="last" if last else "early",
+        compiler_params=params(8 if last else 20),
         cost_estimate=pl.CostEstimate(flops=32_000_000, bytes_accessed=1 << 20, transcendentals=0),
-    )(ids, lengths, spread, order, left, own, *mine, *theirs)
+    )(ids, lengths, spread, order, left, partial if last else weights, *rights)
 
 
 def mix_kernel(blocks, kept, scale, in_ref, out_ref):
@@ -224,34 +216,43 @@
     )(folded)
 
 
-def project_kernel(ids_ref, kept_ref, other_ref, first_ref, second_ref, out_ref):
+def project_kernel(ids_ref, kept_ref, other_ref, first_ref, weights_ref, out_ref, second_ref, sems):
     _, width = first_ref.shape
-    part = min(512, width)
-    for order, (rows_ref, weights_ref) in enumerate(((kept_ref, first_ref), (other_ref, second_ref))):
+    count = sems.shape[0]
+    part = width // count
+    copies = [
+        pltpu.make_async_copy(
+            weights_ref.at[1 - ids_ref[0], :, pl.ds(i * part, part)], second_ref.at[:, pl.ds(i * part, part)], sems.at[i]
+        )
+        for i in range(count)
+    ]
+    for copy in copies:
+        copy.start()
+    for order, (rows_ref, from_ref) in enumerate(((kept_ref, first_ref), (other_ref, second_ref))):
         layer = ids_ref[0] if order == 0 else 1 - ids_ref[0]
-
-        @pl.loop(0, width // part)
-        def _(step):
-            col = pl.multiple_of(step * part, part)
-            out_ref[:, pl.ds(pl.multiple_of(layer * width + col, 128), part)] = jnp.dot(
-                rows_ref[...], weights_ref[:, pl.ds(col, part)], preferred_element_type=F32
+        for i in range(count):
+            if order == 1:
+                copies[i].wait()
+            out_ref[:, pl.ds(pl.multiple_of(layer * width + i * part, 128), part)] = jnp.dot(
+                rows_ref[...], from_ref[:, i * part:(i + 1) * part], preferred_element_type=F32
             ).astype(out_ref.dtype)
 
 
-def project(ids, kept, other, first, second):
+def project(ids, kept, other, first, weights):
     documents, depth = kept.shape
     width = first.shape[1]
     return pl.pallas_call(
         project_kernel,
-        in_specs=[SMEM_SPEC] + [VMEM_SPEC] * 4,
+        in_specs=[SMEM_SPEC] + [VMEM_SPEC] * 3 + [HBM_SPEC],
         out_specs=VMEM_SPEC,
         out_shape=jax.ShapeDtypeStruct((documents, 2 * width), BF16),
+        scratch_shapes=[pltpu.VMEM((depth, width), BF16), pltpu.SemaphoreType.DMA((4,))],
         name="project",
-        compiler_params=params(2),
+        compiler_params=params(20),
         cost_estimate=pl.CostEstimate(
             flops=4 * documents * depth * width, bytes_accessed=4 * depth * width, transcendentals=0
         ),
-    )(ids, kept, other, first, second)
+    )(ids, kept, other, first, weights)
 
 
 def exchange(rows):
@@ -274,22 +275,25 @@
     ids = jnp.stack([my_half, my_block]).astype(jnp.int32)
     weights = projection.reshape(layers, rows_block * kept_cols, projection.shape[3])
 
-    routes = [(2 * b, 2 * b + 2) for b in range(blocks - 1)] + [(2 * b + 3, 2 * b + 1) for b in range(blocks - 1)]
-    own = out_factors[:, 0]
-    mine, theirs = [], []
-    for _ in range(1, blocks):
-        got = lax.ppermute(mine[-1] if mine else own, ("blk", "sub"), routes)
-        mine.append(got)
-        theirs.append(lax.ppermute(got, "sub", [(0, 1), (1, 0)]))
+    rights = {0: lax.dynamic_index_in_dim(out_factors[:, 0], my_half, 0, keepdims=False)}
+    bit = blocks // 2
+    while bit:
+        for mask in list(rights):
+            rights[mask | bit] = lax.ppermute(rights[mask], "blk", [(b, b ^ bit) for b in range(blocks)])
+        bit //= 2
     left = lax.dynamic_index_in_dim(in_factors[:, 0], my_half, 0, keepdims=False)
     left = exchange(left.T.reshape(blocks, rows_block, tok_local))
     spread, order = prepare(ids, signs, kept_cols)
-    first = fetch(ids, weights, 0)
-    second = fetch(ids, weights, 1)
-    folded = exchange(fold(ids, lengths, spread, order, left, own, mine, theirs, kept_cols))
+    masks = range(blocks)
+    early, late = masks[:-1], masks[-1:]
+    partial, first = fold(
+        ids, lengths, spread, order, left, [rights[m] for m in early], early, kept_cols, weights=weights
+    )
+    folded = fold(ids, lengths, spread, order, left, [rights[m] for m in late], late, kept_cols, partial=partial)
+    folded = exchange(folded)
     kept = exchange(mix(folded, blocks, kept_cols, scale))
     other = lax.ppermute(kept, "sub", [(0, 1), (1, 0)])
-    terms = exchange(project(ids, kept, other, first, second))
+    terms = exchange(project(ids, kept, other, first, weights))
     terms = terms.reshape(blocks, docs, layers, weights.shape[2]).astype(F32)
     return jnp.sum(terms, axis=0)[None]
 

time: 135 us -> 94.9 us (0.70)
  waiting for transfers between devices: 23.8 us -> 11.5 us
  starting transfers between devices: 21 us -> 9.52 us
  local copies, waits for them, and re-layouts: 19.3 us -> 8.15 us
  Pallas kernels: 30.6 us -> 23.2 us
  blocking collectives: 39.5 us -> 41.8 us
    unnamed x18 -> x10, local copies, waits for them, and re-layouts: 17.7 us -> 5.55 us
    ppermute x6 -> x3, starting transfers between devices: 15.1 us -> 6.12 us  [shards(): lax.ppermute(rights[mask], 'blk', [(b, b ^ bit) for b in range(blocks)])]
    ppermute x6 -> x3, waiting for transfers between devices: 19 us -> 10 us  [shards(): lax.ppermute(rights[mask], 'blk', [(b, b ^ bit) for b in range(blocks)])]
    pallas_call x4 -> x3, Pallas kernels: 28.2 us -> 20.8 us  [the longest x2 10.6 us: fold(): pl.pallas_call(functools.partial(fold_kernel, kept, tile, masks, last), g...]
    all_to_all x1, waiting for transfers between devices: 4.8 us -> 0.01 us  [exchange(): return lax.all_to_all(rows, 'blk', split_axis=0, concat_axis=0, tiled=True)]
    all_to_all x1, starting transfers between devices: 5.88 us -> 3.4 us  [exchange(): return lax.all_to_all(rows, 'blk', split_axis=0, concat_axis=0, tiled=True)]
    all_to_all x3, blocking collectives: 39.5 us -> 41.8 us  [exchange(): return lax.all_to_all(rows, 'blk', split_axis=0, concat_axis=0, tiled=True)]
    ppermute x1, waiting for transfers between devices: 0.01 us -> 1.53 us  [shards(): other = lax.ppermute(kept, 'sub', [(0, 1), (1, 0)])]
  transfers between devices with their start and end apart: 8 -> 5, of which waited for: 4 -> 3; matrix products, arithmetic and copies ran while one was open for 1% -> 2% of each run, Pallas kernels for 11% -> 9%
where the time goes in v4:
time: 94.9 us; the launch traced here: 94.4 us
  blocking collectives  41.8 us (44%)
  Pallas kernels  23.2 us (24%)
  waiting for transfers between devices  11.5 us (12%)
  starting transfers between devices  9.52 us (10%)
  local copies, waits for them, and re-layouts  8.15 us (9%)
    all_to_all x3, blocking collectives, exchange(): return lax.all_to_all(rows, 'blk', split_axis=0, concat_axis=0, tiled=True)  41.8 us
    pallas_call x2, Pallas kernels, fold(): pl.pallas_call(functools.partial(fold_kernel, kept, tile, masks, last), g...  10.6 us
    pallas_call x1, Pallas kernels, project(): pl.pallas_call(project_kernel, in_specs=[SMEM_SPEC] + [VMEM_SPEC] * 3 + [...  10.2 us
    ppermute x3, waiting for transfers between devices, shards(): lax.ppermute(rights[mask], 'blk', [(b, b ^ bit) for b in range(blocks)])  10 us
    ppermute x3, starting transfers between devices, shards(): lax.ppermute(rights[mask], 'blk', [(b, b ^ bit) for b in range(blocks)])  6.12 us
    unnamed x10, local copies, waits for them, and re-layouts  5.55 us
    all_to_all x1, starting transfers between devices, exchange(): return lax.all_to_all(rows, 'blk', split_axis=0, concat_axis=0, tiled=True)  3.4 us
  transfers between devices with their start and end apart: 5, of which 3 were waited for; matrix products, arithmetic and copies ran while one was open for 2% of the time, Pallas kernels for 9%

profile of v4, /device:TPU:0, one launch (start us, length us, event | category | flops | bytes accessed | tf_op | source)
XLA Modules:
  0.0 94.4 jit_solution(4099111187348428738)
XLA Ops:
  0.0 0.0 copy-start
  0.0 1.0 %copy-done = bf16[2,1,128,1024]{3,2,1,0:T(8,128)(2,1)S(1)} copy-done((bf16[2,1,128,1024]{3,2,1,0:T(8,128)(2,1)S(1)}, bf16[2,1,128,1024]{3,2,1,0:T(8,128)(2,1)}, u32[]{:S(2)}) %copy-start) | copy-done | bytes 524312
  1.0 0.0 copy-start.4
  1.1 4.1 %collective-permute-start.1 = (bf16[128,1024]{1,0:T(8,128)(2,1)S(1)}, bf16[128,1024]{1,0:T(8,128)(2,1)S(1)}, u32[]{:S(2)}, u32[]{:S(2)}) collective-permute-start(bf16[128,1024]{1,0:T(8,128)(2,1)S(1)} %dynamic-slice_bitcast_fusion.refs_6_), channel_id=1, source_target_pairs={{0,8},{4,12},{8,0},{12,4},{1,9},{5,13},{9,1},{13,5},{2,10},{6,14},... | collective-permute-start | bytes 786440 | tf_op jit(solution)/shard_map/ppermute | solution.py:282
  5.2 1.0 %dynamic-slice_bitcast_fusion.1 = bf16[1024,128]{0,1:T(8,128)(2,1)S(1)} fusion(bf16[2,1,128,1024]{3,2,1,0:T(8,128)(2,1)} %param.5, s32[]{:T(128)S(6)} %select_n.5), kind=kLoop, calls=%fused_computation.2 | loop fusion | bytes 524292 | tf_op jit(solution)/shard_map/transpose | solution.py:285
  6.2 0.8 copy.6
  7.0 3.4 %all-to-all-start = ((bf16[4,256,128]{2,1,0:T(8,128)(2,1)}), bf16[4,256,128]{2,1,0:T(8,128)(2,1)S(1)}, u32[]{:S(2)}, u32[]{:S(2)}) async-start(bf16[4,256,128]{2,1,0:T(8,128)(2,1)} %bitcast.4), calls=%async_computation | async-start | bytes 524288 | tf_op jit(solution)/shard_map/all_to_all | solution.py:259
  10.4 2.0 %collective-permute-start = (bf16[128,1024]{1,0:T(8,128)(2,1)S(1)}, bf16[128,1024]{1,0:T(8,128)(2,1)}, u32[]{:S(2)}, u32[]{:S(2)}) collective-permute-start(bf16[128,1024]{1,0:T(8,128)(2,1)S(1)} %dynamic-slice_bitcast_fusion.refs_6_), channel_id=1, source_target_pairs={{0,4},{4,0},{8,12},{12,8},{1,5},{5,1},{9,13},{13,9},{2,6},{6,2},{1... | collective-permute-start | bytes 786440 | tf_op jit(solution)/shard_map/ppermute | solution.py:282
  12.4 8.4 %collective-permute-done.1.refs_8_ = bf16[128,1024]{1,0:T(8,128)(2,1)S(1)} collective-permute-done((bf16[128,1024]{1,0:T(8,128)(2,1)S(1)}, bf16[128,1024]{1,0:T(8,128)(2,1)S(1)}, u32[]{:S(2)}, u32[]{:S(2)}) %collective-permute-start.1) | collective-permute-done | bytes 262176 | tf_op jit(solution)/shard_map/ppermute | solution.py:282
  20.8 0.0 collective-permute-start.2
  20.8 0.1 pad_add_fusion.ids_ref.refs_0_
  20.9 0.0 copy-start.3
  20.9 1.6 %copy-done.3 = s32[2,256,1024]{2,1,0:T(8,128)S(1)} copy-done((s32[2,256,1024]{2,1,0:T(8,128)S(1)}, s32[2,256,1024]{2,1,0:T(8,128)}, u32[]{:S(2)}) %copy-start.3) | copy-done | bytes 2097176
  22.5 1.7 %prepare.1 = (bf16[4,4,256,256]{3,2,1,0:T(8,128)(2,1)S(1)}, bf16[1024,1024]{1,0:T(8,128)(2,1)S(1)}) custom-call(s32[2]{0:T(128)S(1)} %pad_add_fusion.ids_ref.refs_0_, s32[2,256,1024]{2,1,0:T(8,128)S(1)} %copy-done.3), custom_call_target="tpu_custom_call" | custom-call | flops 16000000 | bytes 2097152 | tf_op jit(solution)/shard_map/prepare/pallas_call | solution.py:58
  24.2 0.0 copy-start.1
  24.2 1.3 %copy-done.1 = bf16[1024,1024]{1,0:T(8,128)(2,1)} copy-done((bf16[1024,1024]{1,0:T(8,128)(2,1)}, bf16[1024,1024]{1,0:T(8,128)(2,1)S(1)}, u32[]{:S(2)}) %copy-start.1) | copy-done | bytes 2097176
  25.6 1.6 %collective-permute-done.refs_7_ = bf16[128,1024]{1,0:T(8,128)(2,1)} collective-permute-done((bf16[128,1024]{1,0:T(8,128)(2,1)S(1)}, bf16[128,1024]{1,0:T(8,128)(2,1)}, u32[]{:S(2)}, u32[]{:S(2)}) %collective-permute-start) | collective-permute-done | bytes 262176 | tf_op jit(solution)/shard_map/ppermute | solution.py:282
  27.1 0.0 all-to-all-done.refs_4_
  27.2 0.0 copy-done.4
  27.2 0.0 copy-start.2
  27.2 1.6 %copy-done.2 = bf16[1024,1024]{1,0:T(8,128)(2,1)S(1)} copy-done((bf16[1024,1024]{1,0:T(8,128)(2,1)S(1)}, bf16[1024,1024]{1,0:T(8,128)(2,1)}, u32[]{:S(2)}) %copy-start.2) | copy-done | bytes 2097176
  28.7 7.0 %early.1 = (f32[32,4096]{1,0:T(8,128)S(1)}, bf16[4096,2048]{1,0:T(8,128)(2,1)S(1)}) custom-call(s32[2]{0:T(128)S(1)} %pad_add_fusion.ids_ref.refs_0_, s32[1,32]{1,0:T(1,128)S(1)} %copy-done.4, bf16[4,4,256,256]{3,2,1,0:T(8,128)(2,1)S(1)} %get-tuple-element.9.refs_2_, bf16[1024,1024]{1,0:T(8,128)(2,1)S(1)} %copy-done.2, ...), custom_call_target="tpu_custom_call" | custom-call | flops 32000000 | bytes 1048576 | tf_op jit(solution)/shard_map/early/pallas_call | solution.py:160
  35.8 0.0 collective-permute-done.2.refs_6_
  35.8 3.6 %last.1 = f32[32,4096]{1,0:T(8,128)S(1)} custom-call(s32[2]{0:T(128)S(1)} %pad_add_fusion.ids_ref.refs_0_, s32[1,32]{1,0:T(1,128)S(1)} %copy-done.4, bf16[4,4,256,256]{3,2,1,0:T(8,128)(2,1)S(1)} %get-tuple-element.9.refs_2_, bf16[1024,1024]{1,0:T(8,128)(2,1)S(1)} %copy-done.2, bf16[4,256,128]{2,1,0:T(8,128)(2,1)S(1)} %all-to-all-done.refs_4_, ...), custom_call_target="tpu_custom_call" | custom-call | flops 32000000 | bytes 1048576 | tf_op jit(solution)/shard_map/last/pallas_call | solution.py:160
  39.4 18.9 %all_to_all.36 = f32[4,8,4096]{2,1,0:T(8,128)S(1)} all-to-all(f32[4,8,4096]{2,1,0:T(8,128)S(1)} %bitcast.15), channel_id=1, replica_groups=mesh['parts'=2,'blk'=4,'dp'=2,'sub'=2] {'blk'}, dimensions={0} | all-to-all | bytes 1048576 | tf_op jit(solution)/shard_map/all_to_all | solution.py:259
  58.4 0.6 mix.1
  59.0 11.0 %all_to_all.37 = bf16[4,8,4096]{2,1,0:T(8,128)(2,1)S(1)} all-to-all(bf16[4,8,4096]{2,1,0:T(8,128)(2,1)S(1)} %bitcast.20), channel_id=1, replica_groups=mesh['parts'=2,'blk'=4,'dp'=2,'sub'=2] {'blk'}, dimensions={0} | all-to-all | bytes 524288 | tf_op jit(solution)/shard_map/all_to_all | solution.py:259
  70.0 0.0 collective-permute-start.3
  70.0 1.5 %collective-permute-done.3.other_ref = bf16[32,4096]{1,0:T(8,128)(2,1)S(1)} collective-permute-done((bf16[32,4096]{1,0:T(8,128)(2,1)S(1)}, bf16[32,4096]{1,0:T(8,128)(2,1)S(1)}, u32[]{:S(2)}, u32[]{:S(2)}) %collective-permute-start.3) | collective-permute-done | bytes 262176 | tf_op jit(solution)/shard_map/ppermute | solution.py:295
  71.5 10.2 %project.1 = bf16[32,4096]{1,0:T(8,128)(2,1)S(1)} custom-call(s32[2]{0:T(128)S(1)} %pad_add_fusion.ids_ref.refs_0_, bf16[32,4096]{1,0:T(8,128)(2,1)S(1)} %bitcast.18, bf16[32,4096]{1,0:T(8,128)(2,1)S(1)} %collective-permute-done.3.other_ref, bf16[4096,2048]{1,0:T(8,128)(2,1)S(1)} %get-tuple-element.12.first_ref, bf16[2,4096,2048]{2,1,0:T(8,128)(2,1)} %bitcast.22), custom_call_target="tpu_custom_call" | custom-call | flops 1073741824 | bytes 33554432 | tf_op jit(solution)/shard_map/project/pallas_call | solution.py:244
  81.7 11.8 %all_to_all.38 = bf16[4,8,4096]{2,1,0:T(8,128)(2,1)S(1)} all-to-all(bf16[4,8,4096]{2,1,0:T(8,128)(2,1)S(1)} %bitcast.19), channel_id=1, replica_groups=mesh['parts'=2,'blk'=4,'dp'=2,'sub'=2] {'blk'}, dimensions={0} | all-to-all | bytes 524288 | tf_op jit(solution)/shard_map/all_to_all | solution.py:259
  93.6 0.8 broadcast_in_dim.3
  (2 shorter events, 0.1 us)
Async XLA Ops:
  0.0 1.0 %copy-start = (bf16[2,1,128,1024]{3,2,1,0:T(8,128)(2,1)S(1)}, bf16[2,1,128,1024]{3,2,1,0:T(8,128)(2,1)}, u32[]{:S(2)}) copy-start(bf16[2,1,128,1024]{3,2,1,0:T(8,128)(2,1)} %param.6) | copy-start | bytes 1572868
  1.0 26.1 %copy-start.4 = (s32[1,32]{1,0:T(1,128)S(1)}, s32[1,32]{1,0:T(1,128)}, u32[]{:S(2)}) copy-start(s32[1,32]{1,0:T(1,128)} %refs_1_.3) | copy-start | bytes 388
  1.1 19.8 %collective-permute-start.1 = (bf16[128,1024]{1,0:T(8,128)(2,1)S(1)}, bf16[128,1024]{1,0:T(8,128)(2,1)S(1)}, u32[]{:S(2)}, u32[]{:S(2)}) collective-permute-start(bf16[128,1024]{1,0:T(8,128)(2,1)S(1)} %dynamic-slice_bitcast_fusion.refs_6_), channel_id=1, source_target_pairs={{0,8},{4,12},{8,0},{12,4},{1,9},{5,13},{9,1},{13,5},{2,10},{6,14},... | collective-permute-start | bytes 786440 | tf_op jit(solution)/shard_map/ppermute | solution.py:282
  7.0 20.1 %all-to-all-start = ((bf16[4,256,128]{2,1,0:T(8,128)(2,1)}), bf16[4,256,128]{2,1,0:T(8,128)(2,1)S(1)}, u32[]{:S(2)}, u32[]{:S(2)}) async-start(bf16[4,256,128]{2,1,0:T(8,128)(2,1)} %bitcast.4), calls=%async_computation | async-start | bytes 524288 | tf_op jit(solution)/shard_map/all_to_all | solution.py:259
  10.4 16.7 %collective-permute-start = (bf16[128,1024]{1,0:T(8,128)(2,1)S(1)}, bf16[128,1024]{1,0:T(8,128)(2,1)}, u32[]{:S(2)}, u32[]{:S(2)}) collective-permute-start(bf16[128,1024]{1,0:T(8,128)(2,1)S(1)} %dynamic-slice_bitcast_fusion.refs_6_), channel_id=1, source_target_pairs={{0,4},{4,0},{8,12},{12,8},{1,5},{5,1},{9,13},{13,9},{2,6},{6,2},{1... | collective-permute-start | bytes 786440 | tf_op jit(solution)/shard_map/ppermute | solution.py:282
  20.8 14.9 %collective-permute-start.2 = (bf16[128,1024]{1,0:T(8,128)(2,1)S(1)}, bf16[128,1024]{1,0:T(8,128)(2,1)}, u32[]{:S(2)}, u32[]{:S(2)}) collective-permute-start(bf16[128,1024]{1,0:T(8,128)(2,1)S(1)} %collective-permute-done.1.refs_8_), channel_id=1, source_target_pairs={{0,4},{4,0},{8,12},{12,8},{1,5},{5,1},{9,13},{13,9},{2,6},{6,2},{1... | collective-permute-start | bytes 786440 | tf_op jit(solution)/shard_map/ppermute | solution.py:282
  20.9 1.6 %copy-start.3 = (s32[2,256,1024]{2,1,0:T(8,128)S(1)}, s32[2,256,1024]{2,1,0:T(8,128)}, u32[]{:S(2)}) copy-start(s32[2,256,1024]{2,1,0:T(8,128)} %signs_ref.1) | copy-start | bytes 6291460
  24.2 1.3 %copy-start.1 = (bf16[1024,1024]{1,0:T(8,128)(2,1)}, bf16[1024,1024]{1,0:T(8,128)(2,1)S(1)}, u32[]{:S(2)}) copy-start(bf16[1024,1024]{1,0:T(8,128)(2,1)S(1)} %get-tuple-element.10.refs_3_) | copy-start | bytes 6291460
  27.2 1.6 %copy-start.2 = (bf16[1024,1024]{1,0:T(8,128)(2,1)S(1)}, bf16[1024,1024]{1,0:T(8,128)(2,1)}, u32[]{:S(2)}) copy-start(bf16[1024,1024]{1,0:T(8,128)(2,1)} %copy-done.1) | copy-start | bytes 6291460
  70.0 1.5 %collective-permute-start.3 = (bf16[32,4096]{1,0:T(8,128)(2,1)S(1)}, bf16[32,4096]{1,0:T(8,128)(2,1)S(1)}, u32[]{:S(2)}, u32[]{:S(2)}) collective-permute-start(bf16[32,4096]{1,0:T(8,128)(2,1)S(1)} %bitcast.17), channel_id=1, source_target_pairs={{0,1},{1,0},{2,3},{3,2},{4,5},{5,4},{6,7},{7,6},{8,9},{9,8},{10,11... | collective-permute-start | bytes 786440 | tf_op jit(solution)/shard_map/ppermute | solution.py:295
